TPU v7x, 32 devices: a whole 2x2x4 slice. The times are simulated.
32 devices in a mesh: grp: 2 (over y), col: 4 (over z), row: 2 (over x), dir: 2 (over core).
Axes of the slice: x: 2, y: 2, z: 4, core: 2. Of those that a mesh axis runs over, the one named last changes fastest.
Arguments:
- slopes_in: bfloat16 [512, 8192], P(None, ('grp', 'col')), parts along dimension 1, may hold values from -6 to 6
- basis_left: bfloat16 [12, 16, 256, 256], P(('row', 'dir'), 'col'), may hold values from -0.09375 to 0.09375
- basis_right: bfloat16 [12, 16, 256, 256], P(('row', 'dir'), 'col'), may hold values from -0.375 to 0.375
- rank_blocks: int32 [12, 16], P(('row', 'dir'), 'col'), may hold values from 1 to 4
- tile_owner: int32 [16], replicated, may hold values from 0 to 15, each once
- footprint: int32 [4, 4, 4, 2048], P(('row', 'dir')), may hold values from 0 to 767
- trace_weight: float32 [4, 4, 4, 2048], P(('row', 'dir')), may hold values from 0 to 0.5
- fitting: bfloat16 [2048, 4096], P(None, 'col'), may hold values from -0.125 to 0.125
Outputs:
- commands: bfloat16 [4, 1024, 4096], P(('row', 'dir'), 'grp', 'col'), parts along dimension 1
There are 2 independent parts, one for each index of `grp`. A program takes and returns all parts, laid end to end along the dimension named above; an argument that names none is the same for every part. Nothing has to cross between parts.
Inputs may be any that keep to these rules, and one draw needn't show every extreme that they name: rank_blocks[i, k] is the number of leading blocks of 64 columns of tile (i, k) that are live. `tile_owner`: each slope block appears in exactly one tile slot. `footprint`: indices into one layer's points.
All inputs are finite; a program needn't handle non-finite values.
Results may differ from a plain program's by a relative error of at most 0.0064.
Values may be sent and summed in bfloat16 or wider, within the bound.
No kernel may reach another device: no remote copies, remote signals or barrier semaphores. Data moves between devices by JAX's collectives and lax.ppermute only.
A program may use at most 128 MiB of HBM per device.

v0:
```python
import functools

import jax
import jax.numpy as jnp
from jax import lax
from jax.experimental import pallas as pl
from jax.experimental.pallas import tpu as pltpu
from jax.sharding import PartitionSpec as P


RB = 64


def shift(value, axis, step):
    count = lax.axis_size(axis)
    return lax.ppermute(value, axis, [(i, (i + step) % count) for i in range(count)])


def wide(
    slopes_in, basis_left, basis_right, rank_blocks, tile_owner, footprint, trace_weight, fitting
):
    frames = slopes_in.shape[0]
    rows_here, slots_here, tile_size, rank_cols = basis_left.shape
    columns, rows, dirs = lax.axis_size("col"), lax.axis_size("row"), lax.axis_size("dir")
    col, row, direction = lax.axis_index("col"), lax.axis_index("row"), lax.axis_index("dir")
    group = rows * dirs
    mine = row * dirs + direction
    piece = frames // (columns * group)
    width = slots_here * tile_size
    points = rows_here * tile_size

    pieces = slopes_in.reshape(columns, group, piece, width)
    held = []
    for s in range(columns):
        part = lax.dynamic_index_in_dim(pieces, (col + s) % columns, 0, keepdims=False)
        part = lax.dynamic_index_in_dim(part, mine, 0, keepdims=False)
        held.append(part if s == 0 else shift(part, "col", s))
    blocks = jnp.stack(held).reshape(columns, piece, slots_here, tile_size)
    blocks = blocks.transpose(0, 2, 1, 3).reshape(columns * slots_here, piece, tile_size)
    owner_col, owner_slot = tile_owner // slots_here, tile_owner % slots_here
    place = ((col - owner_col) % columns) * slots_here + owner_slot
    got = []
    for s in range(columns):
        want = lax.dynamic_slice_in_dim(place, ((col + s) % columns) * slots_here, slots_here, 0)
        part = jnp.take(blocks, want, axis=0)
        got.append(part if s == 0 else shift(part, "col", s))
    chosen = jnp.stack(got, axis=1)
    chosen = jnp.stack([chosen] + [shift(chosen, "row", -t) for t in range(1, rows)], axis=2)
    chosen = jnp.stack([chosen] + [shift(chosen, "dir", -t) for t in range(1, dirs)], axis=3)
    chosen = chosen.reshape(slots_here, frames, tile_size)

    live = jnp.arange(rank_cols, dtype=jnp.int32) // RB < rank_blocks[:, :, None]
    coeffs = jnp.einsum("kfn,iknr->ikfr", chosen, basis_right, preferred_element_type=jnp.float32)
    coeffs = jnp.where(live[:, :, None, :], coeffs, 0.0).astype(jnp.bfloat16)
    summed = jnp.einsum("ikfr,iknr->fin", coeffs, basis_left, preferred_element_type=jnp.float32)
    summed = summed.astype(jnp.bfloat16).reshape(columns, frames // columns, points)
    total = summed[0].astype(jnp.float32)
    for s in range(1, columns):
        total = total + shift(summed[s], "col", -s).astype(jnp.float32)
    layer_block = total.astype(jnp.bfloat16)

    layer_count, taps, pupil_count = footprint.shape[1:]
    per_layer = points * group // layer_count
    shifts = (jnp.arange(layer_count, dtype=jnp.int32) * per_layer)[:, None, None]
    flat = (footprint[0] + shifts).reshape(layer_count * taps, pupil_count)
    weight = trace_weight[0].reshape(layer_count * taps, pupil_count)
    if per_layer % points == 0:
        near = True
    else:
        near = False

    def tap_matrix(dr, dd):
        q = ((row + dr) % rows) * dirs + (direction + dd) % dirs
        f, w = flat, weight
        if near:
            first = (q * points // per_layer) * taps
            f = lax.dynamic_slice_in_dim(flat, first, taps, 0)
            w = lax.dynamic_slice_in_dim(weight, first, taps, 0)
        here = q * points + jnp.arange(points, dtype=jnp.int32)
        out = jnp.zeros((points, pupil_count), jnp.float32)
        for c in range(f.shape[0]):
            out = out + jnp.where(here[:, None] == f[c][None, :], w[c][None, :], 0.0)
        return out.astype(jnp.bfloat16)

    matrix = [[tap_matrix(dr, dd) for dd in range(dirs)] for dr in range(rows)]

    share = frames // columns
    order = layer_block.reshape(rows, dirs, piece, points)
    result = []
    for s in range(columns):
        here = order if s == 0 else shift(order, "col", s)
        pupil = jnp.zeros((share, pupil_count), jnp.float32)
        for dr in range(rows):
            far = here if dr == 0 else jnp.roll(shift(here, "row", -dr), dr, axis=0)
            for dd in range(dirs):
                block = far if dd == 0 else jnp.roll(shift(far, "dir", -dd), dd, axis=1)
                pupil = pupil + jnp.dot(
                    block.reshape(share, points),
                    matrix[dr][dd],
                    preferred_element_type=jnp.float32,
                )
        pupil = pupil.astype(jnp.bfloat16)
        result.append(
            jnp.dot(pupil, fitting, preferred_element_type=jnp.float32).astype(jnp.bfloat16)
        )
    commands = jnp.stack(result).reshape(columns, rows, dirs, piece, -1)
    commands = jnp.take(commands, (col - jnp.arange(columns)) % columns, axis=0)
    commands = jnp.take(commands, (jnp.arange(rows) - row) % rows, axis=1)
    commands = jnp.take(commands, (jnp.arange(dirs) - direction) % dirs, axis=2)
    return commands.reshape(1, frames, -1)


WHOLE = pl.BlockSpec(memory_space=pltpu.VMEM)
SCALARS = pl.BlockSpec(memory_space=pltpu.SMEM)


def tap_kernel(per_layer, dr, dd, foot_ref, weight_ref, out_ref):
    points, pupil_count = out_ref.shape
    taps = foot_ref.shape[1]
    first = ((lax.axis_index("row") ^ dr) * 2 + (lax.axis_index("dir") ^ dd)) * points
    layer = first // per_layer
    base = first - layer * per_layer
    wide = 256
    tall = 16
    block = 256

    def lanes(j, _):
        cols = pl.ds(pl.multiple_of(j * wide, wide), wide)
        weight = [
            jnp.broadcast_to(
                weight_ref[layer, c : c + 1, cols].astype(jnp.bfloat16), (tall, wide)
            )
            for c in range(taps)
        ]
        spot = lax.broadcasted_iota(jnp.int32, (tall, wide), 0)
        spot = spot.astype(jnp.float32).astype(jnp.bfloat16)
        zero = jnp.zeros((tall, wide), jnp.bfloat16)
        for b in range(points // block):
            foot = []
            for c in range(taps):
                near = foot_ref[layer, c : c + 1, cols] - (base + b * block)
                near = jnp.where((near >= 0) & (near < block), near, -1)
                near = near.astype(jnp.float32).astype(jnp.bfloat16)
                foot.append(jnp.broadcast_to(near, (tall, wide)))
            for i in range(block // tall):
                here = spot + jnp.bfloat16(i * tall)
                total = jnp.where(here == foot[0], weight[0], zero)
                for c in range(1, taps):
                    total = total + jnp.where(here == foot[c], weight[c], zero)
                first = b * block + i * tall
                out_ref[first : first + tall, cols] = total
        return 0

    lax.fori_loop(0, pupil_count // wide, lanes, 0)


def tap_matrix(footprint, weight, dr, dd, points, per_layer):
    pupil_count = footprint.shape[2]
    return pl.pallas_call(
        functools.partial(tap_kernel, per_layer, dr, dd),
        out_shape=jax.ShapeDtypeStruct((points, pupil_count), jnp.bfloat16),
        in_specs=[WHOLE, WHOLE],
        out_specs=WHOLE,
        cost_estimate=pl.CostEstimate(
            flops=400 * points * pupil_count,
            bytes_accessed=2 * points * pupil_count,
            transcendentals=0,
        ),
        compiler_params=pltpu.CompilerParams(vmem_limit_bytes=8 << 20),
        name="tap_matrix",
    )(footprint, weight)


def pick_kernel(blocks, place_ref, *refs):
    columns = (len(refs) - 1) // 2
    held_refs, got_refs, held = refs[:columns], refs[columns:-1], refs[-1]
    _, width = held_refs[0].shape
    slots_here = blocks // columns
    tile_size = width // slots_here
    col = place_ref[0]
    for s in range(columns):
        held[s] = held_refs[s][...]
    for s in range(columns):
        for j in range(slots_here):
            block = place_ref[3 + (col ^ s) * slots_here + j]
            source = col ^ (block // slots_here)
            lane = pl.multiple_of((block % slots_here) * tile_size, tile_size)
            got_refs[s][:, j * tile_size : (j + 1) * tile_size] = held[
                source, :, pl.ds(lane, tile_size)
            ]


def pick_blocks(place, blocks, held):
    columns = len(held)
    return pl.pallas_call(
        functools.partial(pick_kernel, blocks),
        out_shape=[jax.ShapeDtypeStruct(held[0].shape, held[0].dtype)] * columns,
        in_specs=[SCALARS] + [WHOLE] * columns,
        out_specs=[WHOLE] * columns,
        scratch_shapes=[pltpu.VMEM((columns,) + held[0].shape, held[0].dtype)],
        cost_estimate=pl.CostEstimate(flops=1 << 20, bytes_accessed=1 << 19, transcendentals=0),
        compiler_params=pltpu.CompilerParams(vmem_limit_bytes=4 << 20),
        name="pick_blocks",
    )(place, *held)


def partial_kernel(place_ref, own_ref, other_ref, right_ref, left_ref, *refs):
    out_refs, all_ref = refs[:-1], refs[-1]
    rows_here, slots_here, tile_size, rank_cols = left_ref.shape
    columns, piece, _ = own_ref.shape
    here = place_ref[2]
    rows = 2 * columns * piece
    ranks = 3 + columns * slots_here
    column = lax.broadcasted_iota(jnp.int32, (rows, rank_cols), 1) // RB
    for which, ref in enumerate((own_ref, other_ref)):
        spot = here if which == 0 else 1 - here
        for s in range(columns):
            first = pl.multiple_of((2 * s + spot) * piece, piece)
            all_ref[pl.ds(first, piece), :] = ref[s]
    for i in range(rows_here):
        total = None
        for k in range(slots_here):
            coeffs = jnp.dot(
                all_ref[:, k * tile_size : (k + 1) * tile_size],
                right_ref[i, k],
                preferred_element_type=jnp.float32,
            )
            coeffs = jnp.where(column < place_ref[ranks + i * slots_here + k], coeffs, 0.0).astype(jnp.bfloat16)
            term = lax.dot_general(
                coeffs,
                left_ref[i, k],
                (((1,), (1,)), ((), ())),
                preferred_element_type=jnp.float32,
            )
            total = term if total is None else total + term
        total = total.astype(jnp.bfloat16)
        for s in range(columns):
            out_refs[s][:, i * tile_size : (i + 1) * tile_size] = total[
                2 * s * piece : 2 * (s + 1) * piece
            ]


def partial_sums(place, own, other, right, left):
    rows_here, slots_here, tile_size, rank_cols = left.shape
    columns, piece, width = own.shape
    out = jax.ShapeDtypeStruct((2 * piece, rows_here * tile_size), jnp.bfloat16)
    return pl.pallas_call(
        partial_kernel,
        out_shape=[out] * columns,
        in_specs=[SCALARS] + [WHOLE] * 4,
        out_specs=[WHOLE] * columns,
        scratch_shapes=[pltpu.VMEM((2 * columns * piece, width), jnp.bfloat16)],
        cost_estimate=pl.CostEstimate(
            flops=8 * columns * piece * rows_here * slots_here * tile_size * rank_cols,
            bytes_accessed=4 * right.size,
            transcendentals=0,
        ),
        compiler_params=pltpu.CompilerParams(vmem_limit_bytes=12 << 20),
        name="partial_sums",
    )(place, own, other, right, left)


def command_kernel(wide, shares, *refs):
    refs = list(refs)
    parts = [refs.pop(0) for _ in range(4)]
    matrix = [refs.pop(0) for _ in range(4)]
    fit_ref = refs.pop(0)
    early = len(shares) - 1
    done = [refs.pop(0) for _ in range(early)]
    out_ref, field_ref, pupil_ref = refs[:3]
    share, points = parts[0].shape
    half = share // 2
    sent = []

    def send(source, s, h, cols):
        spot = (lax.axis_index("col") ^ s) * 2 + (lax.axis_index("row") ^ h)
        spot = pl.multiple_of(spot * half, half)
        copy = pltpu.make_async_copy(
            source.at[h * half : (h + 1) * half, cols],
            out_ref.at[pl.ds(spot, half), cols],
            refs[4].at[len(sent)],
        )
        copy.start()
        sent.append(copy)

    for s, ref in zip(shares, done):
        for h in range(2):
            send(ref, s, h, slice(None))
    for j, ref in enumerate(parts):
        cols = slice(j * points, (j + 1) * points)
        if j % 2 == 0:
            field_ref[:, cols] = ref[...]
        else:
            field_ref[:half, cols] = ref[half:]
            field_ref[half:, cols] = ref[:half]

    for j in range(pupil_ref.shape[1] // wide):
        cols = slice(j * wide, (j + 1) * wide)
        total = None
        for c in range(4):
            term = jnp.dot(
                field_ref[:, c * points : (c + 1) * points],
                matrix[c][:, cols],
                preferred_element_type=jnp.float32,
            )
            total = term if total is None else total + term
        pupil_ref[:, cols] = total.astype(jnp.bfloat16)

    value_ref = refs[3] if early else out_ref
    for j in range(fit_ref.shape[1] // wide):
        cols = slice(j * wide, (j + 1) * wide)
        value_ref[:, cols] = jnp.dot(
            pupil_ref[...], fit_ref[:, cols], preferred_element_type=jnp.float32
        ).astype(jnp.bfloat16)
        for h in range(2 if early else 0):
            send(value_ref, shares[-1], h, cols)
    for copy in sent:
        copy.wait()


def command_rows(parts, matrix, fitting, early=(), shares=(0,), frames=0):
    share, points = parts[0].shape
    pupil_count, acts = fitting.shape
    wide = 256
    operands = list(parts) + list(matrix) + [fitting] + list(early)
    scratch = [
        pltpu.VMEM((share, 4 * points), jnp.bfloat16),
        pltpu.VMEM((share, pupil_count), jnp.bfloat16),
    ]
    if early:
        scratch.append(pltpu.VMEM((share, acts), jnp.bfloat16))
        scratch.append(pltpu.SemaphoreType.DMA((2 * len(early) + 2 * (acts // wide),)))
    return pl.pallas_call(
        functools.partial(command_kernel, wide, shares),
        out_shape=jax.ShapeDtypeStruct((frames if early else share, acts), jnp.bfloat16),
        in_specs=[WHOLE] * len(operands),
        out_specs=pl.BlockSpec(memory_space=pltpu.HBM) if early else WHOLE,
        scratch_shapes=scratch,
        cost_estimate=pl.CostEstimate(
            flops=2 * share * pupil_count * (4 * points + acts),
            bytes_accessed=4 * share * acts,
            transcendentals=0,
        ),
        compiler_params=pltpu.CompilerParams(vmem_limit_bytes=26 << 20),
        name="command_rows",
    )(*operands)


def pass_kernel(own_ref, other_ref, out_ref):
    col = lax.axis_index("col")
    outer = (col == 0) | (col == lax.axis_size("col") - 1)

    @pl.when(outer)
    def _():
        out_ref[...] = own_ref[...]

    @pl.when(jnp.logical_not(outer))
    def _():
        out_ref[...] = other_ref[...]


def pass_on(own, other):
    return pl.pallas_call(
        pass_kernel,
        out_shape=jax.ShapeDtypeStruct(own.shape, own.dtype),
        in_specs=[WHOLE, WHOLE],
        out_specs=WHOLE,
        cost_estimate=pl.CostEstimate(flops=1 << 18, bytes_accessed=1 << 19, transcendentals=0),
        compiler_params=pltpu.CompilerParams(vmem_limit_bytes=2 << 20),
        name="pass_on",
    )(own, other)


def swap(value, axis, step):
    return lax.ppermute(value, axis, [(i, i ^ step) for i in range(lax.axis_size(axis))])


def after(values, *others):
    flat, tree = jax.tree.flatten((values, others))
    return jax.tree.unflatten(tree, lax.optimization_barrier(flat))


def narrow(
    slopes_in, basis_left, basis_right, rank_blocks, tile_owner, footprint, trace_weight, fitting
):
    frames = slopes_in.shape[0]
    rows_here, _, tile_size, _ = basis_left.shape
    columns, rows, dirs = lax.axis_size("col"), lax.axis_size("row"), lax.axis_size("dir")
    col, row, direction = lax.axis_index("col"), lax.axis_index("row"), lax.axis_index("dir")
    place = jnp.stack([col, row, direction]).astype(jnp.int32)
    place = jnp.concatenate([place, tile_owner, rank_blocks.reshape(-1)])
    group = rows * dirs
    mine = row * dirs + direction
    piece = frames // (columns * group)
    points = rows_here * tile_size
    per_layer = points * group // footprint.shape[1]

    def taps(dr, dd):
        return tap_matrix(footprint[0], trace_weight[0], dr, dd, points, per_layer)

    matrix = [taps(0, 0), taps(1, 0), taps(0, 1), taps(1, 1)]

    def exchange(parts):
        return [parts[0]] + [swap(parts[s], "col", s) for s in range(1, columns)]

    held = []
    for s in range(columns):
        spot = ((col ^ s) * group + mine) * piece
        held.append(lax.dynamic_slice_in_dim(slopes_in, spot, piece, 0))
    held = exchange(held)
    held, (matrix[0],) = after(held, matrix[0])
    got = exchange(pick_blocks(place, tile_owner.shape[0], held))
    got, (matrix[1],) = after(got, matrix[1])
    own = jnp.stack(got)
    over = swap(own, "row", 1)
    sibling = swap(own, "dir", 1)
    near_sums = partial_sums(place, own, sibling, basis_right, basis_left)
    near_in = exchange(near_sums)
    far_sums = partial_sums(place, over, swap(over, "dir", 1), basis_right, basis_left)
    far_in = exchange(far_sums)

    def add(parts):
        total = parts[0].astype(jnp.float32)
        for part in parts[1:]:
            total = total + part.astype(jnp.float32)
        return total.astype(jnp.bfloat16)

    near_in, _ = after(near_in, far_sums)
    layers = [jnp.concatenate([add(near_in), add(far_in)], axis=0)] * columns
    layers[3] = swap(layers[0], "col", 3)
    layers[1] = swap(layers[0], "col", 1)
    onward = pass_on(layers[0], layers[3])
    layers[2] = lax.ppermute(onward, "col", [(0, 2), (1, 0), (2, 3), (3, 1)])

    early = []
    shares = (0, 3, 1, 2)
    for s in shares:
        here = layers[s]
        over = swap(here, "row", 1)
        field = [here, over, swap(here, "dir", 1), swap(over, "dir", 1)]
        if s != shares[-1]:
            early.append(command_rows(field, matrix, fitting))
        else:
            commands = command_rows(field, matrix, fitting, early, shares, frames)
    return commands[None]


def shards(*args):
    frames = args[0].shape[0]
    points = args[1].shape[0] * args[1].shape[2]
    columns, rows, dirs = lax.axis_size("col"), lax.axis_size("row"), lax.axis_size("dir")
    per_layer = points * rows * dirs // args[5].shape[1]
    piece = frames // (columns * rows * dirs)
    fits = piece % 16 == 0 and per_layer % points == 0 and points % 256 == 0
    if rows == 2 and dirs == 2 and columns == 4 and fits:
        return narrow(*args)
    return wide(*args)


def solution(mesh):
    placed = (
        P(None, ("grp", "col")),
        P(("row", "dir"), "col", None, None),
        P(("row", "dir"), "col", None, None),
        P(("row", "dir"), "col"),
        P(),
        P(("row", "dir"), None, None, None),
        P(("row", "dir"), None, None, None),
        P(None, "col"),
    )
    return jax.shard_map(
        shards,
        mesh=mesh,
        in_specs=placed,
        out_specs=P(("row", "dir"), "grp", "col"),
        check_vma=False,
    )
```

profile of v0, /device:TPU:0, one launch (start us, length us, event | category | flops | bytes accessed | tf_op | source)
XLA Modules:
  0.0 87.9 jit_solution(18272362396508361387)
XLA Ops:
  1.0 5.1 %collective-permute-start.2 = (bf16[32,1024]{1,0:T(8,128)(2,1)S(1)}, bf16[32,1024]{1,0:T(8,128)(2,1)S(1)}, u32[]{:S(2)}, u32[]{:S(2)}) collective-permute-start(bf16[32,1024]{1,0:T(8,128)(2,1)S(1)} %get-tuple-element.57), channel_id=1, source_target_pairs={{0,12},{4,8},{8,4},{12,0},{1,13},{5,9},{9,5},{13,1},{2,14},{6,10},... | collective-permute-start | bytes 196616 | tf_op jit(solution)/shard_map/ppermute | solution.py:375
  10.1 1.5 %tap_matrix.4.refs_4_ = bf16[768,2048]{1,0:T(8,128)(2,1)S(1)} custom-call(s32[4,4,2048]{2,1,0:T(4,128)S(1)} %bitcast.10, f32[4,4,2048]{2,1,0:T(4,128)S(1)} %bitcast.14), custom_call_target="tpu_custom_call" | custom-call | flops 629145600 | bytes 3145728 | tf_op jit(solution)/shard_map/tap_matrix/pallas_call | solution.py:159
  12.4 1.6 %collective-permute-start.3 = (bf16[32,1024]{1,0:T(8,128)(2,1)S(1)}, bf16[32,1024]{1,0:T(8,128)(2,1)S(1)}, u32[]{:S(2)}, u32[]{:S(2)}) collective-permute-start(bf16[32,1024]{1,0:T(8,128)(2,1)S(1)} %get-tuple-element.36), channel_id=1, source_target_pairs={{0,4},{4,0},{8,12},{12,8},{1,5},{5,1},{9,13},{13,9},{2,6},{6,2},{1... | collective-permute-start | bytes 196616 | tf_op jit(solution)/shard_map/ppermute | solution.py:375
  14.0 2.6 %collective-permute-start.4 = (bf16[32,1024]{1,0:T(8,128)(2,1)S(1)}, bf16[32,1024]{1,0:T(8,128)(2,1)S(1)}, u32[]{:S(2)}, u32[]{:S(2)}) collective-permute-start(bf16[32,1024]{1,0:T(8,128)(2,1)S(1)} %get-tuple-element.37), channel_id=1, source_target_pairs={{0,8},{4,12},{8,0},{12,4},{1,9},{5,13},{9,1},{13,5},{2,10},{6,14},... | collective-permute-start | bytes 196616 | tf_op jit(solution)/shard_map/ppermute | solution.py:375
  16.9 1.5 %tap_matrix.5.refs_5_ = bf16[768,2048]{1,0:T(8,128)(2,1)S(1)} custom-call(s32[4,4,2048]{2,1,0:T(4,128)S(1)} %bitcast.11, f32[4,4,2048]{2,1,0:T(4,128)S(1)} %bitcast.15), custom_call_target="tpu_custom_call" | custom-call | flops 629145600 | bytes 3145728 | tf_op jit(solution)/shard_map/tap_matrix/pallas_call | solution.py:159
  18.4 2.1 %collective-permute-done.4 = bf16[32,1024]{1,0:T(8,128)(2,1)S(1)} collective-permute-done((bf16[32,1024]{1,0:T(8,128)(2,1)S(1)}, bf16[32,1024]{1,0:T(8,128)(2,1)S(1)}, u32[]{:S(2)}, u32[]{:S(2)}) %collective-permute-start.4) | collective-permute-done | bytes 65568 | tf_op jit(solution)/shard_map/ppermute | solution.py:375
  20.5 2.2 %collective-permute-done.5 = bf16[32,1024]{1,0:T(8,128)(2,1)S(1)} collective-permute-done((bf16[32,1024]{1,0:T(8,128)(2,1)S(1)}, bf16[32,1024]{1,0:T(8,128)(2,1)S(1)}, u32[]{:S(2)}, u32[]{:S(2)}) %collective-permute-start.5) | collective-permute-done | bytes 65568 | tf_op jit(solution)/shard_map/ppermute | solution.py:375
  22.7 1.6 %collective-permute-start.10 = (bf16[4,32,1024]{2,1,0:T(8,128)(2,1)S(1)}, bf16[4,32,1024]{2,1,0:T(8,128)(2,1)S(1)}, u32[]{:S(2)}, u32[]{:S(2)}) collective-permute-start(bf16[4,32,1024]{2,1,0:T(8,128)(2,1)S(1)} %pad_maximum_fusion.own_ref), channel_id=1, source_target_pairs={{0,2},{2,0},{1,3},{3,1},{4,6},{6,4},{5,7},{7,5},{8,10},{10,8},{9,1... | collective-permute-start | bytes 786440 | tf_op jit(solution)/shard_map/ppermute | solution.py:375
  24.3 4.9 %collective-permute-done.10.own_ref = bf16[4,32,1024]{2,1,0:T(8,128)(2,1)S(1)} collective-permute-done((bf16[4,32,1024]{2,1,0:T(8,128)(2,1)S(1)}, bf16[4,32,1024]{2,1,0:T(8,128)(2,1)S(1)}, u32[]{:S(2)}, u32[]{:S(2)}) %collective-permute-start.10) | collective-permute-done | bytes 262176 | tf_op jit(solution)/shard_map/ppermute | solution.py:375
  29.2 1.8 %partial_sums.2 = (bf16[64,768]{1,0:T(8,128)(2,1)S(1)}, bf16[64,768]{1,0:T(8,128)(2,1)S(1)}, bf16[64,768]{1,0:T(8,128)(2,1)S(1)}, bf16[64,768]{1,0:T(8,128)(2,1)S(1)}) custom-call(s32[31]{0:T(128)S(1)} %concatenate.6.place_ref, bf16[4,32,1024]{2,1,0:T(8,128)(2,1)S(1)} %pad_maximum_fusion.own_ref, bf16[4,32,1024]{2,1,0:T(8,128)(2,1)S(1)} %collective-permute-done.6.other_ref, ...), custom_call_target="tpu_custom_call" | custom-call | flops 805306368 | bytes 3145728 | tf_op jit(solution)/shard_map/partial_sums/pallas_call | solution.py:247
  32.6 2.9 %collective-permute-start.9 = (bf16[64,768]{1,0:T(8,128)(2,1)S(1)}, bf16[64,768]{1,0:T(8,128)(2,1)S(1)}, u32[]{:S(2)}, u32[]{:S(2)}) collective-permute-start(bf16[64,768]{1,0:T(8,128)(2,1)S(1)} %get-tuple-element.46), channel_id=1, source_target_pairs={{0,12},{4,8},{8,4},{12,0},{1,13},{5,9},{9,5},{13,1},{2,14},{6,10},... | collective-permute-start | bytes 294920 | tf_op jit(solution)/shard_map/ppermute | solution.py:375
  35.5 1.8 %partial_sums.3 = (bf16[64,768]{1,0:T(8,128)(2,1)S(1)}, bf16[64,768]{1,0:T(8,128)(2,1)S(1)}, bf16[64,768]{1,0:T(8,128)(2,1)S(1)}, bf16[64,768]{1,0:T(8,128)(2,1)S(1)}) custom-call(s32[31]{0:T(128)S(1)} %concatenate.6.place_ref, bf16[4,32,1024]{2,1,0:T(8,128)(2,1)S(1)} %collective-permute-done.10.own_ref, ...), custom_call_target="tpu_custom_call" | custom-call | flops 805306368 | bytes 3145728 | tf_op jit(solution)/shard_map/partial_sums/pallas_call | solution.py:247
  37.3 1.5 %collective-permute-start.13 = (bf16[64,768]{1,0:T(8,128)(2,1)S(1)}, bf16[64,768]{1,0:T(8,128)(2,1)S(1)}, u32[]{:S(2)}, u32[]{:S(2)}) collective-permute-start(bf16[64,768]{1,0:T(8,128)(2,1)S(1)} %get-tuple-element.49), channel_id=1, source_target_pairs={{0,8},{4,12},{8,0},{12,4},{1,9},{5,13},{9,1},{13,5},{2,10},{6,14},... | collective-permute-start | bytes 294920 | tf_op jit(solution)/shard_map/ppermute | solution.py:375
  38.8 2.9 %collective-permute-start.14 = (bf16[64,768]{1,0:T(8,128)(2,1)S(1)}, bf16[64,768]{1,0:T(8,128)(2,1)S(1)}, u32[]{:S(2)}, u32[]{:S(2)}) collective-permute-start(bf16[64,768]{1,0:T(8,128)(2,1)S(1)} %get-tuple-element.50), channel_id=1, source_target_pairs={{0,12},{4,8},{8,4},{12,0},{1,13},{5,9},{9,5},{13,1},{2,14},{6,10},... | collective-permute-start | bytes 294920 | tf_op jit(solution)/shard_map/ppermute | solution.py:375
  42.0 1.6 %collective-permute-done.12 = bf16[64,768]{1,0:T(8,128)(2,1)S(1)} collective-permute-done((bf16[64,768]{1,0:T(8,128)(2,1)S(1)}, bf16[64,768]{1,0:T(8,128)(2,1)S(1)}, u32[]{:S(2)}, u32[]{:S(2)}) %collective-permute-start.12) | collective-permute-done | bytes 98336 | tf_op jit(solution)/shard_map/ppermute | solution.py:375
  43.6 6.8 %collective-permute-done.13 = bf16[64,768]{1,0:T(8,128)(2,1)S(1)} collective-permute-done((bf16[64,768]{1,0:T(8,128)(2,1)S(1)}, bf16[64,768]{1,0:T(8,128)(2,1)S(1)}, u32[]{:S(2)}, u32[]{:S(2)}) %collective-permute-start.13) | collective-permute-done | bytes 98336 | tf_op jit(solution)/shard_map/ppermute | solution.py:375
  50.5 2.3 %collective-permute-start.26 = (bf16[128,768]{1,0:T(8,128)(2,1)S(1)}, bf16[128,768]{1,0:T(8,128)(2,1)S(1)}, u32[]{:S(2)}, u32[]{:S(2)}) collective-permute-start(bf16[128,768]{1,0:T(8,128)(2,1)S(1)} %pad_maximum_fusion.1.own_ref.refs_0_), channel_id=1, source_target_pairs={{0,4},{4,0},{8,12},{12,8},{1,5},{5,1},{9,13},{13,9},{2,6},{6,2},{1... | collective-permute-start | bytes 589832 | tf_op jit(solution)/shard_map/ppermute | solution.py:375
  52.8 1.5 %collective-permute-start.20 = (bf16[128,768]{1,0:T(8,128)(2,1)S(1)}, bf16[128,768]{1,0:T(8,128)(2,1)S(1)}, u32[]{:S(2)}, u32[]{:S(2)}) collective-permute-start(bf16[128,768]{1,0:T(8,128)(2,1)S(1)} %pad_maximum_fusion.1.own_ref.refs_0_), channel_id=1, source_target_pairs={{0,2},{2,0},{1,3},{3,1},{4,6},{6,4},{5,7},{7,5},{8,10},{10,8},{9,1... | collective-permute-start | bytes 589832 | tf_op jit(solution)/shard_map/ppermute | solution.py:375
  54.2 1.9 %collective-permute-start.15 = (bf16[128,768]{1,0:T(8,128)(2,1)S(1)}, bf16[128,768]{1,0:T(8,128)(2,1)S(1)}, u32[]{:S(2)}, u32[]{:S(2)}) collective-permute-start(bf16[128,768]{1,0:T(8,128)(2,1)S(1)} %pad_maximum_fusion.1.own_ref.refs_0_), channel_id=1, source_target_pairs={{0,12},{4,8},{8,4},{12,0},{1,13},{5,9},{9,5},{13,1},{2,14},{6,10},... | collective-permute-start | bytes 589832 | tf_op jit(solution)/shard_map/ppermute | solution.py:375
  56.1 1.9 %collective-permute-done.26.refs_0_ = bf16[128,768]{1,0:T(8,128)(2,1)S(1)} collective-permute-done((bf16[128,768]{1,0:T(8,128)(2,1)S(1)}, bf16[128,768]{1,0:T(8,128)(2,1)S(1)}, u32[]{:S(2)}, u32[]{:S(2)}) %collective-permute-start.26) | collective-permute-done | bytes 196640 | tf_op jit(solution)/shard_map/ppermute | solution.py:375
  58.0 1.5 %collective-permute-start.27 = (bf16[128,768]{1,0:T(8,128)(2,1)S(1)}, bf16[128,768]{1,0:T(8,128)(2,1)S(1)}, u32[]{:S(2)}, u32[]{:S(2)}) collective-permute-start(bf16[128,768]{1,0:T(8,128)(2,1)S(1)} %collective-permute-done.26.refs_0_), channel_id=1, source_target_pairs={{0,2},{2,0},{1,3},{3,1},{4,6},{6,4},{5,7},{7,5},{8,10},{10,8},{9,1... | collective-permute-start | bytes 589832 | tf_op jit(solution)/shard_map/ppermute | solution.py:375
  59.5 3.5 %collective-permute-done.15.other_ref.refs_0_ = bf16[128,768]{1,0:T(8,128)(2,1)S(1)} collective-permute-done((bf16[128,768]{1,0:T(8,128)(2,1)S(1)}, bf16[128,768]{1,0:T(8,128)(2,1)S(1)}, u32[]{:S(2)}, u32[]{:S(2)}) %collective-permute-start.15) | collective-permute-done | bytes 196640 | tf_op jit(solution)/shard_map/ppermute | solution.py:375
  63.1 2.0 %collective-permute-start.16 = (bf16[128,768]{1,0:T(8,128)(2,1)S(1)}, bf16[128,768]{1,0:T(8,128)(2,1)S(1)}, u32[]{:S(2)}, u32[]{:S(2)}) collective-permute-start(bf16[128,768]{1,0:T(8,128)(2,1)S(1)} %pass_on.1), channel_id=1, source_target_pairs={{0,8},{4,0},{8,12},{12,4},{1,9},{5,1},{9,13},{13,5},{2,10},{6,2},{... | collective-permute-start | bytes 589832 | tf_op jit(solution)/shard_map/ppermute | solution.py:433
  65.1 1.5 %tap_matrix.7.refs_7_ = bf16[768,2048]{1,0:T(8,128)(2,1)S(1)} custom-call(s32[4,4,2048]{2,1,0:T(4,128)S(1)} %bitcast.12, f32[4,4,2048]{2,1,0:T(4,128)S(1)} %bitcast.16), custom_call_target="tpu_custom_call" | custom-call | flops 629145600 | bytes 3145728 | tf_op jit(solution)/shard_map/tap_matrix/pallas_call | solution.py:159
  66.6 1.5 %tap_matrix.6.refs_6_ = bf16[768,2048]{1,0:T(8,128)(2,1)S(1)} custom-call(s32[4,4,2048]{2,1,0:T(4,128)S(1)} %bitcast.13, f32[4,4,2048]{2,1,0:T(4,128)S(1)} %bitcast.17), custom_call_target="tpu_custom_call" | custom-call | flops 629145600 | bytes 3145728 | tf_op jit(solution)/shard_map/tap_matrix/pallas_call | solution.py:159
  69.2 1.6 %collective-permute-start.17 = (bf16[128,768]{1,0:T(8,128)(2,1)S(1)}, bf16[128,768]{1,0:T(8,128)(2,1)S(1)}, u32[]{:S(2)}, u32[]{:S(2)}) collective-permute-start(bf16[128,768]{1,0:T(8,128)(2,1)S(1)} %collective-permute-done.16.refs_0_), channel_id=1, source_target_pairs={{0,2},{2,0},{1,3},{3,1},{4,6},{6,4},{5,7},{7,5},{8,10},{10,8},{9,1... | collective-permute-start | bytes 589832 | tf_op jit(solution)/shard_map/ppermute | solution.py:375
  70.8 2.4 %command_rows.4.refs_9_ = bf16[128,1024]{1,0:T(8,128)(2,1)S(1)} custom-call(bf16[128,768]{1,0:T(8,128)(2,1)S(1)} %pad_maximum_fusion.1.own_ref.refs_0_, bf16[128,768]{1,0:T(8,128)(2,1)S(1)} %collective-permute-done.20.refs_1_, bf16[128,768]{1,0:T(8,128)(2,1)S(1)} %collective-permute-done.21.refs_2_, bf16[128,768]{1,0:T(8,128)(2,1)S(1)} %collective-permute-done.22.refs_3_, ...), custom_call_target="tpu_custom_call" | custom-call | flops 2147483648 | bytes 524288 | tf_op jit(solution)/shard_map/command_rows/pallas_call | solution.py:333
  73.4 3.1 %collective-permute-done.23.refs_1_ = bf16[128,768]{1,0:T(8,128)(2,1)S(1)} collective-permute-done((bf16[128,768]{1,0:T(8,128)(2,1)S(1)}, bf16[128,768]{1,0:T(8,128)(2,1)S(1)}, u32[]{:S(2)}, u32[]{:S(2)}) %collective-permute-start.23) | collective-permute-done | bytes 196640 | tf_op jit(solution)/shard_map/ppermute | solution.py:375
  76.5 3.3 %collective-permute-done.17.refs_1_ = bf16[128,768]{1,0:T(8,128)(2,1)S(1)} collective-permute-done((bf16[128,768]{1,0:T(8,128)(2,1)S(1)}, bf16[128,768]{1,0:T(8,128)(2,1)S(1)}, u32[]{:S(2)}, u32[]{:S(2)}) %collective-permute-start.17) | collective-permute-done | bytes 196640 | tf_op jit(solution)/shard_map/ppermute | solution.py:375
  79.8 2.4 %command_rows.6.refs_11_ = bf16[128,1024]{1,0:T(8,128)(2,1)S(1)} custom-call(bf16[128,768]{1,0:T(8,128)(2,1)S(1)} %collective-permute-done.26.refs_0_, bf16[128,768]{1,0:T(8,128)(2,1)S(1)} %collective-permute-done.27.refs_1_, bf16[128,768]{1,0:T(8,128)(2,1)S(1)} %collective-permute-done.28.refs_2_, bf16[128,768]{1,0:T(8,128)(2,1)S(1)} %collective-permute-done.29.refs_3_, ...), custom_call_target="tpu_custom_call" | custom-call | flops 2147483648 | bytes 524288 | tf_op jit(solution)/shard_map/command_rows/pallas_call | solution.py:333
  82.2 2.4 %command_rows.5.refs_10_ = bf16[128,1024]{1,0:T(8,128)(2,1)S(1)} custom-call(bf16[128,768]{1,0:T(8,128)(2,1)S(1)} %collective-permute-done.15.other_ref.refs_0_, bf16[128,768]{1,0:T(8,128)(2,1)S(1)} %collective-permute-done.23.refs_1_, bf16[128,768]{1,0:T(8,128)(2,1)S(1)} %collective-permute-done.24.refs_2_, ...), custom_call_target="tpu_custom_call" | custom-call | flops 2147483648 | bytes 524288 | tf_op jit(solution)/shard_map/command_rows/pallas_call | solution.py:333
  84.6 3.1 %command_rows.7 = bf16[512,1024]{1,0:T(8,128)(2,1)} custom-call(bf16[128,768]{1,0:T(8,128)(2,1)S(1)} %collective-permute-done.16.refs_0_, bf16[128,768]{1,0:T(8,128)(2,1)S(1)} %collective-permute-done.17.refs_1_, bf16[128,768]{1,0:T(8,128)(2,1)S(1)} %collective-permute-done.18.refs_2_, bf16[128,768]{1,0:T(8,128)(2,1)S(1)} %collective-permute-done.19.refs_3_, ...), custom_call_target="tpu_custom_call" | custom-call | flops 2147483648 | bytes 524288 | tf_op jit(solution)/shard_map/command_rows/pallas_call | solution.py:333
  (61 shorter events, 9.4 us)
Async XLA Ops:
  1.0 10.6 %collective-permute-start.2 = (bf16[32,1024]{1,0:T(8,128)(2,1)S(1)}, bf16[32,1024]{1,0:T(8,128)(2,1)S(1)}, u32[]{:S(2)}, u32[]{:S(2)}) collective-permute-start(bf16[32,1024]{1,0:T(8,128)(2,1)S(1)} %get-tuple-element.57), channel_id=1, source_target_pairs={{0,12},{4,8},{8,4},{12,0},{1,13},{5,9},{9,5},{13,1},{2,14},{6,10},... | collective-permute-start | bytes 196616 | tf_op jit(solution)/shard_map/ppermute | solution.py:375
  6.1 5.5 %collective-permute-start = (bf16[32,1024]{1,0:T(8,128)(2,1)S(1)}, bf16[32,1024]{1,0:T(8,128)(2,1)S(1)}, u32[]{:S(2)}, u32[]{:S(2)}) collective-permute-start(bf16[32,1024]{1,0:T(8,128)(2,1)S(1)} %get-tuple-element.58), channel_id=1, source_target_pairs={{0,4},{4,0},{8,12},{12,8},{1,5},{5,1},{9,13},{13,9},{2,6},{6,2},{1... | collective-permute-start | bytes 196616 | tf_op jit(solution)/shard_map/ppermute | solution.py:375
  6.1 5.6 %collective-permute-start.1 = (bf16[32,1024]{1,0:T(8,128)(2,1)S(1)}, bf16[32,1024]{1,0:T(8,128)(2,1)S(1)}, u32[]{:S(2)}, u32[]{:S(2)}) collective-permute-start(bf16[32,1024]{1,0:T(8,128)(2,1)S(1)} %get-tuple-element.60), channel_id=1, source_target_pairs={{0,8},{4,12},{8,0},{12,4},{1,9},{5,13},{9,1},{13,5},{2,10},{6,14},... | collective-permute-start | bytes 196616 | tf_op jit(solution)/shard_map/ppermute | solution.py:375
  12.4 6.0 %collective-permute-start.3 = (bf16[32,1024]{1,0:T(8,128)(2,1)S(1)}, bf16[32,1024]{1,0:T(8,128)(2,1)S(1)}, u32[]{:S(2)}, u32[]{:S(2)}) collective-permute-start(bf16[32,1024]{1,0:T(8,128)(2,1)S(1)} %get-tuple-element.36), channel_id=1, source_target_pairs={{0,4},{4,0},{8,12},{12,8},{1,5},{5,1},{9,13},{13,9},{2,6},{6,2},{1... | collective-permute-start | bytes 196616 | tf_op jit(solution)/shard_map/ppermute | solution.py:375
  14.0 6.5 %collective-permute-start.4 = (bf16[32,1024]{1,0:T(8,128)(2,1)S(1)}, bf16[32,1024]{1,0:T(8,128)(2,1)S(1)}, u32[]{:S(2)}, u32[]{:S(2)}) collective-permute-start(bf16[32,1024]{1,0:T(8,128)(2,1)S(1)} %get-tuple-element.37), channel_id=1, source_target_pairs={{0,8},{4,12},{8,0},{12,4},{1,9},{5,13},{9,1},{13,5},{2,10},{6,14},... | collective-permute-start | bytes 196616 | tf_op jit(solution)/shard_map/ppermute | solution.py:375
  16.6 6.1 %collective-permute-start.5 = (bf16[32,1024]{1,0:T(8,128)(2,1)S(1)}, bf16[32,1024]{1,0:T(8,128)(2,1)S(1)}, u32[]{:S(2)}, u32[]{:S(2)}) collective-permute-start(bf16[32,1024]{1,0:T(8,128)(2,1)S(1)} %get-tuple-element.38), channel_id=1, source_target_pairs={{0,12},{4,8},{8,4},{12,0},{1,13},{5,9},{9,5},{13,1},{2,14},{6,10},... | collective-permute-start | bytes 196616 | tf_op jit(solution)/shard_map/ppermute | solution.py:375
  22.7 6.4 %collective-permute-start.10 = (bf16[4,32,1024]{2,1,0:T(8,128)(2,1)S(1)}, bf16[4,32,1024]{2,1,0:T(8,128)(2,1)S(1)}, u32[]{:S(2)}, u32[]{:S(2)}) collective-permute-start(bf16[4,32,1024]{2,1,0:T(8,128)(2,1)S(1)} %pad_maximum_fusion.own_ref), channel_id=1, source_target_pairs={{0,2},{2,0},{1,3},{3,1},{4,6},{6,4},{5,7},{7,5},{8,10},{10,8},{9,1... | collective-permute-start | bytes 786440 | tf_op jit(solution)/shard_map/ppermute | solution.py:375
  24.3 4.9 %collective-permute-start.6 = (bf16[4,32,1024]{2,1,0:T(8,128)(2,1)S(1)}, bf16[4,32,1024]{2,1,0:T(8,128)(2,1)S(1)}, u32[]{:S(2)}, u32[]{:S(2)}) collective-permute-start(bf16[4,32,1024]{2,1,0:T(8,128)(2,1)S(1)} %pad_maximum_fusion.own_ref), channel_id=1, source_target_pairs={{0,1},{1,0},{2,3},{3,2},{4,5},{5,4},{6,7},{7,6},{8,9},{9,8},{10,11... | collective-permute-start | bytes 786440 | tf_op jit(solution)/shard_map/ppermute | solution.py:375
  29.2 6.3 %collective-permute-start.11 = (bf16[4,32,1024]{2,1,0:T(8,128)(2,1)S(1)}, bf16[4,32,1024]{2,1,0:T(8,128)(2,1)S(1)}, u32[]{:S(2)}, u32[]{:S(2)}) collective-permute-start(bf16[4,32,1024]{2,1,0:T(8,128)(2,1)S(1)} %collective-permute-done.10.own_ref), channel_id=1, source_target_pairs={{0,1},{1,0},{2,3},{3,2},{4,5},{5,4},{6,7},{7,6},{8,9},{9,8},{10,11... | collective-permute-start | bytes 786440 | tf_op jit(solution)/shard_map/ppermute | solution.py:375
  31.0 34.1 %copy-start.4 = (s32[1,4,4,2048]{3,2,1,0:T(4,128)S(1)}, s32[1,4,4,2048]{3,2,1,0:T(4,128)}, u32[]{:S(2)}) copy-start(s32[1,4,4,2048]{3,2,1,0:T(4,128)} %param.13) | copy-start | bytes 393220
  31.0 34.1 %copy-start.6 = (f32[1,4,4,2048]{3,2,1,0:T(4,128)S(1)}, f32[1,4,4,2048]{3,2,1,0:T(4,128)}, u32[]{:S(2)}) copy-start(f32[1,4,4,2048]{3,2,1,0:T(4,128)} %param.14) | copy-start | bytes 393220
  31.0 7.8 %collective-permute-start.7 = (bf16[64,768]{1,0:T(8,128)(2,1)S(1)}, bf16[64,768]{1,0:T(8,128)(2,1)S(1)}, u32[]{:S(2)}, u32[]{:S(2)}) collective-permute-start(bf16[64,768]{1,0:T(8,128)(2,1)S(1)} %get-tuple-element.44), channel_id=1, source_target_pairs={{0,4},{4,0},{8,12},{12,8},{1,5},{5,1},{9,13},{13,9},{2,6},{6,2},{1... | collective-permute-start | bytes 294920 | tf_op jit(solution)/shard_map/ppermute | solution.py:375
  31.1 10.9 %collective-permute-start.8 = (bf16[64,768]{1,0:T(8,128)(2,1)S(1)}, bf16[64,768]{1,0:T(8,128)(2,1)S(1)}, u32[]{:S(2)}, u32[]{:S(2)}) collective-permute-start(bf16[64,768]{1,0:T(8,128)(2,1)S(1)} %get-tuple-element.45), channel_id=1, source_target_pairs={{0,8},{4,12},{8,0},{12,4},{1,9},{5,13},{9,1},{13,5},{2,10},{6,14},... | collective-permute-start | bytes 294920 | tf_op jit(solution)/shard_map/ppermute | solution.py:375
  32.6 9.4 %collective-permute-start.9 = (bf16[64,768]{1,0:T(8,128)(2,1)S(1)}, bf16[64,768]{1,0:T(8,128)(2,1)S(1)}, u32[]{:S(2)}, u32[]{:S(2)}) collective-permute-start(bf16[64,768]{1,0:T(8,128)(2,1)S(1)} %get-tuple-element.46), channel_id=1, source_target_pairs={{0,12},{4,8},{8,4},{12,0},{1,13},{5,9},{9,5},{13,1},{2,14},{6,10},... | collective-permute-start | bytes 294920 | tf_op jit(solution)/shard_map/ppermute | solution.py:375
  37.2 6.4 %collective-permute-start.12 = (bf16[64,768]{1,0:T(8,128)(2,1)S(1)}, bf16[64,768]{1,0:T(8,128)(2,1)S(1)}, u32[]{:S(2)}, u32[]{:S(2)}) collective-permute-start(bf16[64,768]{1,0:T(8,128)(2,1)S(1)} %get-tuple-element.48), channel_id=1, source_target_pairs={{0,4},{4,0},{8,12},{12,8},{1,5},{5,1},{9,13},{13,9},{2,6},{6,2},{1... | collective-permute-start | bytes 294920 | tf_op jit(solution)/shard_map/ppermute | solution.py:375
  37.3 13.1 %collective-permute-start.13 = (bf16[64,768]{1,0:T(8,128)(2,1)S(1)}, bf16[64,768]{1,0:T(8,128)(2,1)S(1)}, u32[]{:S(2)}, u32[]{:S(2)}) collective-permute-start(bf16[64,768]{1,0:T(8,128)(2,1)S(1)} %get-tuple-element.49), channel_id=1, source_target_pairs={{0,8},{4,12},{8,0},{12,4},{1,9},{5,13},{9,1},{13,5},{2,10},{6,14},... | collective-permute-start | bytes 294920 | tf_op jit(solution)/shard_map/ppermute | solution.py:375
  38.8 11.6 %collective-permute-start.14 = (bf16[64,768]{1,0:T(8,128)(2,1)S(1)}, bf16[64,768]{1,0:T(8,128)(2,1)S(1)}, u32[]{:S(2)}, u32[]{:S(2)}) collective-permute-start(bf16[64,768]{1,0:T(8,128)(2,1)S(1)} %get-tuple-element.50), channel_id=1, source_target_pairs={{0,12},{4,8},{8,4},{12,0},{1,13},{5,9},{9,5},{13,1},{2,14},{6,10},... | collective-permute-start | bytes 294920 | tf_op jit(solution)/shard_map/ppermute | solution.py:375
  50.5 7.6 %collective-permute-start.26 = (bf16[128,768]{1,0:T(8,128)(2,1)S(1)}, bf16[128,768]{1,0:T(8,128)(2,1)S(1)}, u32[]{:S(2)}, u32[]{:S(2)}) collective-permute-start(bf16[128,768]{1,0:T(8,128)(2,1)S(1)} %pad_maximum_fusion.1.own_ref.refs_0_), channel_id=1, source_target_pairs={{0,4},{4,0},{8,12},{12,8},{1,5},{5,1},{9,13},{13,9},{2,6},{6,2},{1... | collective-permute-start | bytes 589832 | tf_op jit(solution)/shard_map/ppermute | solution.py:375
  52.8 6.8 %collective-permute-start.20 = (bf16[128,768]{1,0:T(8,128)(2,1)S(1)}, bf16[128,768]{1,0:T(8,128)(2,1)S(1)}, u32[]{:S(2)}, u32[]{:S(2)}) collective-permute-start(bf16[128,768]{1,0:T(8,128)(2,1)S(1)} %pad_maximum_fusion.1.own_ref.refs_0_), channel_id=1, source_target_pairs={{0,2},{2,0},{1,3},{3,1},{4,6},{6,4},{5,7},{7,5},{8,10},{10,8},{9,1... | collective-permute-start | bytes 589832 | tf_op jit(solution)/shard_map/ppermute | solution.py:375
  54.2 8.8 %collective-permute-start.15 = (bf16[128,768]{1,0:T(8,128)(2,1)S(1)}, bf16[128,768]{1,0:T(8,128)(2,1)S(1)}, u32[]{:S(2)}, u32[]{:S(2)}) collective-permute-start(bf16[128,768]{1,0:T(8,128)(2,1)S(1)} %pad_maximum_fusion.1.own_ref.refs_0_), channel_id=1, source_target_pairs={{0,12},{4,8},{8,4},{12,0},{1,13},{5,9},{9,5},{13,1},{2,14},{6,10},... | collective-permute-start | bytes 589832 | tf_op jit(solution)/shard_map/ppermute | solution.py:375
  56.1 12.1 %collective-permute-start.21 = (bf16[128,768]{1,0:T(8,128)(2,1)S(1)}, bf16[128,768]{1,0:T(8,128)(2,1)S(1)}, u32[]{:S(2)}, u32[]{:S(2)}) collective-permute-start(bf16[128,768]{1,0:T(8,128)(2,1)S(1)} %pad_maximum_fusion.1.own_ref.refs_0_), channel_id=1, source_target_pairs={{0,1},{1,0},{2,3},{3,2},{4,5},{5,4},{6,7},{7,6},{8,9},{9,8},{10,11... | collective-permute-start | bytes 589832 | tf_op jit(solution)/shard_map/ppermute | solution.py:375
  58.0 10.6 %collective-permute-start.27 = (bf16[128,768]{1,0:T(8,128)(2,1)S(1)}, bf16[128,768]{1,0:T(8,128)(2,1)S(1)}, u32[]{:S(2)}, u32[]{:S(2)}) collective-permute-start(bf16[128,768]{1,0:T(8,128)(2,1)S(1)} %collective-permute-done.26.refs_0_), channel_id=1, source_target_pairs={{0,2},{2,0},{1,3},{3,1},{4,6},{6,4},{5,7},{7,5},{8,10},{10,8},{9,1... | collective-permute-start | bytes 589832 | tf_op jit(solution)/shard_map/ppermute | solution.py:375
  59.5 9.2 %collective-permute-start.22 = (bf16[128,768]{1,0:T(8,128)(2,1)S(1)}, bf16[128,768]{1,0:T(8,128)(2,1)S(1)}, u32[]{:S(2)}, u32[]{:S(2)}) collective-permute-start(bf16[128,768]{1,0:T(8,128)(2,1)S(1)} %collective-permute-done.20.refs_1_), channel_id=1, source_target_pairs={{0,1},{1,0},{2,3},{3,2},{4,5},{5,4},{6,7},{7,6},{8,9},{9,8},{10,11... | collective-permute-start | bytes 589832 | tf_op jit(solution)/shard_map/ppermute | solution.py:375
  63.1 6.1 %collective-permute-start.16 = (bf16[128,768]{1,0:T(8,128)(2,1)S(1)}, bf16[128,768]{1,0:T(8,128)(2,1)S(1)}, u32[]{:S(2)}, u32[]{:S(2)}) collective-permute-start(bf16[128,768]{1,0:T(8,128)(2,1)S(1)} %pass_on.1), channel_id=1, source_target_pairs={{0,8},{4,0},{8,12},{12,4},{1,9},{5,1},{9,13},{13,5},{2,10},{6,2},{... | collective-permute-start | bytes 589832 | tf_op jit(solution)/shard_map/ppermute | solution.py:433
  68.1 5.1 %collective-permute-start.28 = (bf16[128,768]{1,0:T(8,128)(2,1)S(1)}, bf16[128,768]{1,0:T(8,128)(2,1)S(1)}, u32[]{:S(2)}, u32[]{:S(2)}) collective-permute-start(bf16[128,768]{1,0:T(8,128)(2,1)S(1)} %collective-permute-done.26.refs_0_), channel_id=1, source_target_pairs={{0,1},{1,0},{2,3},{3,2},{4,5},{5,4},{6,7},{7,6},{8,9},{9,8},{10,11... | collective-permute-start | bytes 589832 | tf_op jit(solution)/shard_map/ppermute | solution.py:375
  68.2 14.0 %collective-permute-start.24 = (bf16[128,768]{1,0:T(8,128)(2,1)S(1)}, bf16[128,768]{1,0:T(8,128)(2,1)S(1)}, u32[]{:S(2)}, u32[]{:S(2)}) collective-permute-start(bf16[128,768]{1,0:T(8,128)(2,1)S(1)} %collective-permute-done.15.other_ref.refs_0_), channel_id=1, source_target_pairs={{0,1},{1,0},{2,3},{3,2},{4,5},{5,4},{6,7},{7,6},{8,9},{9,8},{10,11... | collective-permute-start | bytes 589832 | tf_op jit(solution)/shard_map/ppermute | solution.py:375
  68.7 7.8 %collective-permute-start.23 = (bf16[128,768]{1,0:T(8,128)(2,1)S(1)}, bf16[128,768]{1,0:T(8,128)(2,1)S(1)}, u32[]{:S(2)}, u32[]{:S(2)}) collective-permute-start(bf16[128,768]{1,0:T(8,128)(2,1)S(1)} %collective-permute-done.15.other_ref.refs_0_), channel_id=1, source_target_pairs={{0,2},{2,0},{1,3},{3,1},{4,6},{6,4},{5,7},{7,5},{8,10},{10,8},{9,1... | collective-permute-start | bytes 589832 | tf_op jit(solution)/shard_map/ppermute | solution.py:375
  68.7 11.1 %collective-permute-start.29 = (bf16[128,768]{1,0:T(8,128)(2,1)S(1)}, bf16[128,768]{1,0:T(8,128)(2,1)S(1)}, u32[]{:S(2)}, u32[]{:S(2)}) collective-permute-start(bf16[128,768]{1,0:T(8,128)(2,1)S(1)} %collective-permute-done.27.refs_1_), channel_id=1, source_target_pairs={{0,1},{1,0},{2,3},{3,2},{4,5},{5,4},{6,7},{7,6},{8,9},{9,8},{10,11... | collective-permute-start | bytes 589832 | tf_op jit(solution)/shard_map/ppermute | solution.py:375
  69.2 10.6 %collective-permute-start.17 = (bf16[128,768]{1,0:T(8,128)(2,1)S(1)}, bf16[128,768]{1,0:T(8,128)(2,1)S(1)}, u32[]{:S(2)}, u32[]{:S(2)}) collective-permute-start(bf16[128,768]{1,0:T(8,128)(2,1)S(1)} %collective-permute-done.16.refs_0_), channel_id=1, source_target_pairs={{0,2},{2,0},{1,3},{3,1},{4,6},{6,4},{5,7},{7,5},{8,10},{10,8},{9,1... | collective-permute-start | bytes 589832 | tf_op jit(solution)/shard_map/ppermute | solution.py:375
  73.2 11.4 %collective-permute-start.18 = (bf16[128,768]{1,0:T(8,128)(2,1)S(1)}, bf16[128,768]{1,0:T(8,128)(2,1)S(1)}, u32[]{:S(2)}, u32[]{:S(2)}) collective-permute-start(bf16[128,768]{1,0:T(8,128)(2,1)S(1)} %collective-permute-done.16.refs_0_), channel_id=1, source_target_pairs={{0,1},{1,0},{2,3},{3,2},{4,5},{5,4},{6,7},{7,6},{8,9},{9,8},{10,11... | collective-permute-start | bytes 589832 | tf_op jit(solution)/shard_map/ppermute | solution.py:375
  76.5 5.7 %collective-permute-start.25 = (bf16[128,768]{1,0:T(8,128)(2,1)S(1)}, bf16[128,768]{1,0:T(8,128)(2,1)S(1)}, u32[]{:S(2)}, u32[]{:S(2)}) collective-permute-start(bf16[128,768]{1,0:T(8,128)(2,1)S(1)} %collective-permute-done.23.refs_1_), channel_id=1, source_target_pairs={{0,1},{1,0},{2,3},{3,2},{4,5},{5,4},{6,7},{7,6},{8,9},{9,8},{10,11... | collective-permute-start | bytes 589832 | tf_op jit(solution)/shard_map/ppermute | solution.py:375
  79.8 4.8 %collective-permute-start.19 = (bf16[128,768]{1,0:T(8,128)(2,1)S(1)}, bf16[128,768]{1,0:T(8,128)(2,1)S(1)}, u32[]{:S(2)}, u32[]{:S(2)}) collective-permute-start(bf16[128,768]{1,0:T(8,128)(2,1)S(1)} %collective-permute-done.17.refs_1_), channel_id=1, source_target_pairs={{0,1},{1,0},{2,3},{3,2},{4,5},{5,4},{6,7},{7,6},{8,9},{9,8},{10,11... | collective-permute-start | bytes 589832 | tf_op jit(solution)/shard_map/ppermute | solution.py:375
  (5 other events, 47.8 us)
where the time goes:
time: 88.1 us; the launch traced here: 87.9 us
  starting transfers between devices  32.4 us (37%)
  waiting for transfers between devices  30.2 us (34%)
  Pallas kernels  20.4 us (23%)
  local copies, waits for them, and re-layouts  4.28 us (5%)
    ppermute x29, starting transfers between devices, swap(): lax.ppermute(value, axis, [(i, i ^ step) for i in range(lax.axis_size(axi...  30.4 us
    ppermute x29, waiting for transfers between devices, swap(): lax.ppermute(value, axis, [(i, i ^ step) for i in range(lax.axis_size(axi...  29.9 us
    pallas_call x4, Pallas kernels, command_rows(): pl.pallas_call(functools.partial(command_kernel, wide, shares), out_shape...  10.2 us
    pallas_call x4, Pallas kernels, tap_matrix(): pl.pallas_call(functools.partial(tap_kernel, per_layer, dr, dd), out_shap...  5.99 us
    pallas_call x2, Pallas kernels, partial_sums(): pl.pallas_call(partial_kernel, out_shape=[out] * columns, in_specs=[SCALA...  3.55 us
    ppermute x1, starting transfers between devices, narrow(): layers[2] = lax.ppermute(onward, 'col', [(0, 2), (1, 0), (2, 3), (3, 1)])  1.98 us
    unnamed x14, local copies, waits for them, and re-layouts  1.84 us
  transfers between devices with their start and end apart: 30, of which 12 were waited for; matrix products, arithmetic and copies ran while one was open for 2% of the time, Pallas kernels for 19%

commit v1 on v0

--- a/solution.py
+++ b/solution.py
@@ -260,11 +260,38 @@
     )(place, own, other, right, left)
 
 
-def command_kernel(wide, shares, *refs):
+def half_kernel(wide, own_ref, same_ref, first_ref, second_ref, out_ref):
+    for j in range(out_ref.shape[1] // wide):
+        cols = slice(j * wide, (j + 1) * wide)
+        out_ref[:, cols] = jnp.dot(
+            own_ref[...], first_ref[:, cols], preferred_element_type=jnp.float32
+        ) + jnp.dot(same_ref[...], second_ref[:, cols], preferred_element_type=jnp.float32)
+
+
+def half_pupil(own, same, first, second):
+    share, points = own.shape
+    pupil_count = first.shape[1]
+    return pl.pallas_call(
+        functools.partial(half_kernel, 256),
+        out_shape=jax.ShapeDtypeStruct((share, pupil_count), jnp.float32),
+        in_specs=[WHOLE] * 4,
+        out_specs=WHOLE,
+        cost_estimate=pl.CostEstimate(
+            flops=4 * share * points * pupil_count,
+            bytes_accessed=4 * share * pupil_count,
+            transcendentals=0,
+        ),
+        compiler_params=pltpu.CompilerParams(vmem_limit_bytes=8 << 20),
+        name="half_pupil",
+    )(own, same, first, second)
+
+
+def command_kernel(wide, shares, chunks, *refs):
     refs = list(refs)
-    parts = [refs.pop(0) for _ in range(4)]
-    matrix = [refs.pop(0) for _ in range(4)]
+    parts = [refs.pop(0) for _ in chunks]
+    matrix = [refs.pop(0) for _ in chunks]
     fit_ref = refs.pop(0)
+    base_ref = refs.pop(0) if len(chunks) < 4 else None
     early = len(shares) - 1
     done = [refs.pop(0) for _ in range(early)]
     out_ref, field_ref, pupil_ref = refs[:3]
@@ -288,7 +315,7 @@
             send(ref, s, h, slice(None))
     for j, ref in enumerate(parts):
         cols = slice(j * points, (j + 1) * points)
-        if j % 2 == 0:
+        if chunks[j] % 2 == 0:
             field_ref[:, cols] = ref[...]
         else:
             field_ref[:half, cols] = ref[half:]
@@ -296,8 +323,8 @@
 
     for j in range(pupil_ref.shape[1] // wide):
         cols = slice(j * wide, (j + 1) * wide)
-        total = None
-        for c in range(4):
+        total = None if base_ref is None else base_ref[:, cols]
+        for c in range(len(chunks)):
             term = jnp.dot(
                 field_ref[:, c * points : (c + 1) * points],
                 matrix[c][:, cols],
@@ -318,20 +345,22 @@
         copy.wait()
 
 
-def command_rows(parts, matrix, fitting, early=(), shares=(0,), frames=0):
+def command_rows(parts, matrix, fitting, early=(), shares=(0,), frames=0, base=None):
     share, points = parts[0].shape
     pupil_count, acts = fitting.shape
     wide = 256
-    operands = list(parts) + list(matrix) + [fitting] + list(early)
+    chunks = tuple(range(4)) if base is None else (1, 3)
+    operands = [parts[c] for c in chunks] + [matrix[c] for c in chunks] + [fitting]
+    operands += ([] if base is None else [base]) + list(early)
     scratch = [
-        pltpu.VMEM((share, 4 * points), jnp.bfloat16),
+        pltpu.VMEM((share, len(chunks) * points), jnp.bfloat16),
         pltpu.VMEM((share, pupil_count), jnp.bfloat16),
     ]
     if early:
         scratch.append(pltpu.VMEM((share, acts), jnp.bfloat16))
         scratch.append(pltpu.SemaphoreType.DMA((2 * len(early) + 2 * (acts // wide),)))
     return pl.pallas_call(
-        functools.partial(command_kernel, wide, shares),
+        functools.partial(command_kernel, wide, shares, chunks),
         out_shape=jax.ShapeDtypeStruct((frames if early else share, acts), jnp.bfloat16),
         in_specs=[WHOLE] * len(operands),
         out_specs=pl.BlockSpec(memory_space=pltpu.HBM) if early else WHOLE,
@@ -441,7 +470,8 @@
         if s != shares[-1]:
             early.append(command_rows(field, matrix, fitting))
         else:
-            commands = command_rows(field, matrix, fitting, early, shares, frames)
+            base = half_pupil(field[0], field[2], matrix[0], matrix[2])
+            commands = command_rows(field, matrix, fitting, early, shares, frames, base)
     return commands[None]
 
 

time: 88.1 us -> 88.1 us (level)
    ppermute x1, starting transfers between devices: 1.98 us -> 3.21 us  [narrow(): layers[2] = lax.ppermute(onward, 'col', [(0, 2), (1, 0), (2, 3), (3, 1)])]
    pallas_call x4 -> x5, Pallas kernels: 10.2 us -> 10.4 us  [the longest x4 9.39 us: command_rows(): pl.pallas_call(functools.partial(command_kernel, wide, shares, chunks), o...]
  transfers between devices with their start and end apart: 30 -> 30, of which waited for: 12 -> 10; matrix products, arithmetic and copies ran while one was open for 2% -> 2% of each run, Pallas kernels for 19% -> 20%
where the time goes in v1:
time: 88.1 us; the launch traced here: 87.9 us
  starting transfers between devices  33 us (37%)
  waiting for transfers between devices  29.4 us (33%)
  Pallas kernels  20.6 us (23%)
  local copies, waits for them, and re-layouts  4.28 us (5%)
    ppermute x29, starting transfers between devices, swap(): lax.ppermute(value, axis, [(i, i ^ step) for i in range(lax.axis_size(axi...  29.8 us
    ppermute x29, waiting for transfers between devices, swap(): lax.ppermute(value, axis, [(i, i ^ step) for i in range(lax.axis_size(axi...  29.3 us
    pallas_call x4, Pallas kernels, command_rows(): pl.pallas_call(functools.partial(command_kernel, wide, shares, chunks), o...  9.39 us
    pallas_call x4, Pallas kernels, tap_matrix(): pl.pallas_call(functools.partial(tap_kernel, per_layer, dr, dd), out_shap...  6.01 us
    pallas_call x2, Pallas kernels, partial_sums(): pl.pallas_call(partial_kernel, out_shape=[out] * columns, in_specs=[SCALA...  3.55 us
    ppermute x1, starting transfers between devices, narrow(): layers[2] = lax.ppermute(onward, 'col', [(0, 2), (1, 0), (2, 3), (3, 1)])  3.21 us
    unnamed x14, local copies, waits for them, and re-layouts  1.84 us
  transfers between devices with their start and end apart: 30, of which 10 were waited for; matrix products, arithmetic and copies ran while one was open for 2% of the time, Pallas kernels for 20%

profile of v1, /device:TPU:0, one launch (start us, length us, event | category | flops | bytes accessed | tf_op | source)
XLA Modules:
  0.0 87.9 jit_solution(18397739414607729035)
XLA Ops:
  1.0 3.1 %collective-permute-start = (bf16[32,1024]{1,0:T(8,128)(2,1)S(1)}, bf16[32,1024]{1,0:T(8,128)(2,1)S(1)}, u32[]{:S(2)}, u32[]{:S(2)}) collective-permute-start(bf16[32,1024]{1,0:T(8,128)(2,1)S(1)} %get-tuple-element.58), channel_id=1, source_target_pairs={{0,4},{4,0},{8,12},{12,8},{1,5},{5,1},{9,13},{13,9},{2,6},{6,2},{1... | collective-permute-start | bytes 196616 | tf_op jit(solution)/shard_map/ppermute | solution.py:404
  4.1 2.6 %collective-permute-start.1 = (bf16[32,1024]{1,0:T(8,128)(2,1)S(1)}, bf16[32,1024]{1,0:T(8,128)(2,1)S(1)}, u32[]{:S(2)}, u32[]{:S(2)}) collective-permute-start(bf16[32,1024]{1,0:T(8,128)(2,1)S(1)} %get-tuple-element.60), channel_id=1, source_target_pairs={{0,8},{4,12},{8,0},{12,4},{1,9},{5,13},{9,1},{13,5},{2,10},{6,14},... | collective-permute-start | bytes 196616 | tf_op jit(solution)/shard_map/ppermute | solution.py:404
  10.0 1.5 %tap_matrix.4.first_ref.refs_4_ = bf16[768,2048]{1,0:T(8,128)(2,1)S(1)} custom-call(s32[4,4,2048]{2,1,0:T(4,128)S(1)} %bitcast.10, f32[4,4,2048]{2,1,0:T(4,128)S(1)} %bitcast.14), custom_call_target="tpu_custom_call" | custom-call | flops 629145600 | bytes 3145728 | tf_op jit(solution)/shard_map/tap_matrix/pallas_call | solution.py:159
  11.5 1.2 %collective-permute-done.2.refs_3_ = bf16[32,1024]{1,0:T(8,128)(2,1)S(1)} collective-permute-done((bf16[32,1024]{1,0:T(8,128)(2,1)S(1)}, bf16[32,1024]{1,0:T(8,128)(2,1)S(1)}, u32[]{:S(2)}, u32[]{:S(2)}) %collective-permute-start.2) | collective-permute-done | bytes 65568 | tf_op jit(solution)/shard_map/ppermute | solution.py:404
  13.5 3.1 %collective-permute-start.4 = (bf16[32,1024]{1,0:T(8,128)(2,1)S(1)}, bf16[32,1024]{1,0:T(8,128)(2,1)S(1)}, u32[]{:S(2)}, u32[]{:S(2)}) collective-permute-start(bf16[32,1024]{1,0:T(8,128)(2,1)S(1)} %get-tuple-element.37), channel_id=1, source_target_pairs={{0,8},{4,12},{8,0},{12,4},{1,9},{5,13},{9,1},{13,5},{2,10},{6,14},... | collective-permute-start | bytes 196616 | tf_op jit(solution)/shard_map/ppermute | solution.py:404
  16.6 1.2 %collective-permute-start.5 = (bf16[32,1024]{1,0:T(8,128)(2,1)S(1)}, bf16[32,1024]{1,0:T(8,128)(2,1)S(1)}, u32[]{:S(2)}, u32[]{:S(2)}) collective-permute-start(bf16[32,1024]{1,0:T(8,128)(2,1)S(1)} %get-tuple-element.38), channel_id=1, source_target_pairs={{0,12},{4,8},{8,4},{12,0},{1,13},{5,9},{9,5},{13,1},{2,14},{6,10},... | collective-permute-start | bytes 196616 | tf_op jit(solution)/shard_map/ppermute | solution.py:404
  17.9 1.5 %tap_matrix.5.refs_5_.refs_2_ = bf16[768,2048]{1,0:T(8,128)(2,1)S(1)} custom-call(s32[4,4,2048]{2,1,0:T(4,128)S(1)} %bitcast.11, f32[4,4,2048]{2,1,0:T(4,128)S(1)} %bitcast.15), custom_call_target="tpu_custom_call" | custom-call | flops 629145600 | bytes 3145728 | tf_op jit(solution)/shard_map/tap_matrix/pallas_call | solution.py:159
  19.4 3.3 %collective-permute-done.5 = bf16[32,1024]{1,0:T(8,128)(2,1)S(1)} collective-permute-done((bf16[32,1024]{1,0:T(8,128)(2,1)S(1)}, bf16[32,1024]{1,0:T(8,128)(2,1)S(1)}, u32[]{:S(2)}, u32[]{:S(2)}) %collective-permute-start.5) | collective-permute-done | bytes 65568 | tf_op jit(solution)/shard_map/ppermute | solution.py:404
  22.7 1.6 %collective-permute-start.10 = (bf16[4,32,1024]{2,1,0:T(8,128)(2,1)S(1)}, bf16[4,32,1024]{2,1,0:T(8,128)(2,1)S(1)}, u32[]{:S(2)}, u32[]{:S(2)}) collective-permute-start(bf16[4,32,1024]{2,1,0:T(8,128)(2,1)S(1)} %pad_maximum_fusion.own_ref), channel_id=1, source_target_pairs={{0,2},{2,0},{1,3},{3,1},{4,6},{6,4},{5,7},{7,5},{8,10},{10,8},{9,1... | collective-permute-start | bytes 786440 | tf_op jit(solution)/shard_map/ppermute | solution.py:404
  24.3 4.9 %collective-permute-done.10.own_ref = bf16[4,32,1024]{2,1,0:T(8,128)(2,1)S(1)} collective-permute-done((bf16[4,32,1024]{2,1,0:T(8,128)(2,1)S(1)}, bf16[4,32,1024]{2,1,0:T(8,128)(2,1)S(1)}, u32[]{:S(2)}, u32[]{:S(2)}) %collective-permute-start.10) | collective-permute-done | bytes 262176 | tf_op jit(solution)/shard_map/ppermute | solution.py:404
  29.2 1.8 %partial_sums.2 = (bf16[64,768]{1,0:T(8,128)(2,1)S(1)}, bf16[64,768]{1,0:T(8,128)(2,1)S(1)}, bf16[64,768]{1,0:T(8,128)(2,1)S(1)}, bf16[64,768]{1,0:T(8,128)(2,1)S(1)}) custom-call(s32[31]{0:T(128)S(1)} %concatenate.6.place_ref, bf16[4,32,1024]{2,1,0:T(8,128)(2,1)S(1)} %pad_maximum_fusion.own_ref, bf16[4,32,1024]{2,1,0:T(8,128)(2,1)S(1)} %collective-permute-done.6.other_ref, ...), custom_call_target="tpu_custom_call" | custom-call | flops 805306368 | bytes 3145728 | tf_op jit(solution)/shard_map/partial_sums/pallas_call | solution.py:247
  31.1 1.8 %collective-permute-start.8 = (bf16[64,768]{1,0:T(8,128)(2,1)S(1)}, bf16[64,768]{1,0:T(8,128)(2,1)S(1)}, u32[]{:S(2)}, u32[]{:S(2)}) collective-permute-start(bf16[64,768]{1,0:T(8,128)(2,1)S(1)} %get-tuple-element.45), channel_id=1, source_target_pairs={{0,8},{4,12},{8,0},{12,4},{1,9},{5,13},{9,1},{13,5},{2,10},{6,14},... | collective-permute-start | bytes 294920 | tf_op jit(solution)/shard_map/ppermute | solution.py:404
  32.9 2.6 %collective-permute-start.9 = (bf16[64,768]{1,0:T(8,128)(2,1)S(1)}, bf16[64,768]{1,0:T(8,128)(2,1)S(1)}, u32[]{:S(2)}, u32[]{:S(2)}) collective-permute-start(bf16[64,768]{1,0:T(8,128)(2,1)S(1)} %get-tuple-element.46), channel_id=1, source_target_pairs={{0,12},{4,8},{8,4},{12,0},{1,13},{5,9},{9,5},{13,1},{2,14},{6,10},... | collective-permute-start | bytes 294920 | tf_op jit(solution)/shard_map/ppermute | solution.py:404
  35.5 1.8 %partial_sums.3 = (bf16[64,768]{1,0:T(8,128)(2,1)S(1)}, bf16[64,768]{1,0:T(8,128)(2,1)S(1)}, bf16[64,768]{1,0:T(8,128)(2,1)S(1)}, bf16[64,768]{1,0:T(8,128)(2,1)S(1)}) custom-call(s32[31]{0:T(128)S(1)} %concatenate.6.place_ref, bf16[4,32,1024]{2,1,0:T(8,128)(2,1)S(1)} %collective-permute-done.10.own_ref, ...), custom_call_target="tpu_custom_call" | custom-call | flops 805306368 | bytes 3145728 | tf_op jit(solution)/shard_map/partial_sums/pallas_call | solution.py:247
  37.3 1.8 %collective-permute-start.13 = (bf16[64,768]{1,0:T(8,128)(2,1)S(1)}, bf16[64,768]{1,0:T(8,128)(2,1)S(1)}, u32[]{:S(2)}, u32[]{:S(2)}) collective-permute-start(bf16[64,768]{1,0:T(8,128)(2,1)S(1)} %get-tuple-element.49), channel_id=1, source_target_pairs={{0,8},{4,12},{8,0},{12,4},{1,9},{5,13},{9,1},{13,5},{2,10},{6,14},... | collective-permute-start | bytes 294920 | tf_op jit(solution)/shard_map/ppermute | solution.py:404
  39.1 2.6 %collective-permute-start.14 = (bf16[64,768]{1,0:T(8,128)(2,1)S(1)}, bf16[64,768]{1,0:T(8,128)(2,1)S(1)}, u32[]{:S(2)}, u32[]{:S(2)}) collective-permute-start(bf16[64,768]{1,0:T(8,128)(2,1)S(1)} %get-tuple-element.50), channel_id=1, source_target_pairs={{0,12},{4,8},{8,4},{12,0},{1,13},{5,9},{9,5},{13,1},{2,14},{6,10},... | collective-permute-start | bytes 294920 | tf_op jit(solution)/shard_map/ppermute | solution.py:404
  42.0 1.6 %collective-permute-done.12 = bf16[64,768]{1,0:T(8,128)(2,1)S(1)} collective-permute-done((bf16[64,768]{1,0:T(8,128)(2,1)S(1)}, bf16[64,768]{1,0:T(8,128)(2,1)S(1)}, u32[]{:S(2)}, u32[]{:S(2)}) %collective-permute-start.12) | collective-permute-done | bytes 98336 | tf_op jit(solution)/shard_map/ppermute | solution.py:404
  43.6 6.8 %collective-permute-done.13 = bf16[64,768]{1,0:T(8,128)(2,1)S(1)} collective-permute-done((bf16[64,768]{1,0:T(8,128)(2,1)S(1)}, bf16[64,768]{1,0:T(8,128)(2,1)S(1)}, u32[]{:S(2)}, u32[]{:S(2)}) %collective-permute-start.13) | collective-permute-done | bytes 98336 | tf_op jit(solution)/shard_map/ppermute | solution.py:404
  50.5 2.1 %collective-permute-start.15 = (bf16[128,768]{1,0:T(8,128)(2,1)S(1)}, bf16[128,768]{1,0:T(8,128)(2,1)S(1)}, u32[]{:S(2)}, u32[]{:S(2)}) collective-permute-start(bf16[128,768]{1,0:T(8,128)(2,1)S(1)} %pad_maximum_fusion.1.own_ref.refs_0_), channel_id=1, source_target_pairs={{0,12},{4,8},{8,4},{12,0},{1,13},{5,9},{9,5},{13,1},{2,14},{6,10},... | collective-permute-start | bytes 589832 | tf_op jit(solution)/shard_map/ppermute | solution.py:404
  53.6 1.5 %collective-permute-start.20 = (bf16[128,768]{1,0:T(8,128)(2,1)S(1)}, bf16[128,768]{1,0:T(8,128)(2,1)S(1)}, u32[]{:S(2)}, u32[]{:S(2)}) collective-permute-start(bf16[128,768]{1,0:T(8,128)(2,1)S(1)} %pad_maximum_fusion.1.own_ref.refs_0_), channel_id=1, source_target_pairs={{0,2},{2,0},{1,3},{3,1},{4,6},{6,4},{5,7},{7,5},{8,10},{10,8},{9,1... | collective-permute-start | bytes 589832 | tf_op jit(solution)/shard_map/ppermute | solution.py:404
  55.1 5.0 %collective-permute-done.15.other_ref.refs_0_ = bf16[128,768]{1,0:T(8,128)(2,1)S(1)} collective-permute-done((bf16[128,768]{1,0:T(8,128)(2,1)S(1)}, bf16[128,768]{1,0:T(8,128)(2,1)S(1)}, u32[]{:S(2)}, u32[]{:S(2)}) %collective-permute-start.15) | collective-permute-done | bytes 196640 | tf_op jit(solution)/shard_map/ppermute | solution.py:404
  60.2 3.2 %collective-permute-start.16 = (bf16[128,768]{1,0:T(8,128)(2,1)S(1)}, bf16[128,768]{1,0:T(8,128)(2,1)S(1)}, u32[]{:S(2)}, u32[]{:S(2)}) collective-permute-start(bf16[128,768]{1,0:T(8,128)(2,1)S(1)} %pass_on.1), channel_id=1, source_target_pairs={{0,8},{4,0},{8,12},{12,4},{1,9},{5,1},{9,13},{13,5},{2,10},{6,2},{... | collective-permute-start | bytes 589832 | tf_op jit(solution)/shard_map/ppermute | solution.py:462
  63.4 1.5 %collective-permute-start.27 = (bf16[128,768]{1,0:T(8,128)(2,1)S(1)}, bf16[128,768]{1,0:T(8,128)(2,1)S(1)}, u32[]{:S(2)}, u32[]{:S(2)}) collective-permute-start(bf16[128,768]{1,0:T(8,128)(2,1)S(1)} %collective-permute-done.26.refs_0_), channel_id=1, source_target_pairs={{0,2},{2,0},{1,3},{3,1},{4,6},{6,4},{5,7},{7,5},{8,10},{10,8},{9,1... | collective-permute-start | bytes 589832 | tf_op jit(solution)/shard_map/ppermute | solution.py:404
  64.9 1.5 %tap_matrix.6.refs_7_.refs_3_ = bf16[768,2048]{1,0:T(8,128)(2,1)S(1)} custom-call(s32[4,4,2048]{2,1,0:T(4,128)S(1)} %bitcast.12, f32[4,4,2048]{2,1,0:T(4,128)S(1)} %bitcast.16), custom_call_target="tpu_custom_call" | custom-call | flops 629145600 | bytes 3145728 | tf_op jit(solution)/shard_map/tap_matrix/pallas_call | solution.py:159
  66.4 1.5 %tap_matrix.7.second_ref.refs_6_ = bf16[768,2048]{1,0:T(8,128)(2,1)S(1)} custom-call(s32[4,4,2048]{2,1,0:T(4,128)S(1)} %bitcast.13, f32[4,4,2048]{2,1,0:T(4,128)S(1)} %bitcast.17), custom_call_target="tpu_custom_call" | custom-call | flops 629145600 | bytes 3145728 | tf_op jit(solution)/shard_map/tap_matrix/pallas_call | solution.py:159
  70.0 1.5 %collective-permute-start.17 = (bf16[128,768]{1,0:T(8,128)(2,1)S(1)}, bf16[128,768]{1,0:T(8,128)(2,1)S(1)}, u32[]{:S(2)}, u32[]{:S(2)}) collective-permute-start(bf16[128,768]{1,0:T(8,128)(2,1)S(1)} %collective-permute-done.16.own_ref), channel_id=1, source_target_pairs={{0,2},{2,0},{1,3},{3,1},{4,6},{6,4},{5,7},{7,5},{8,10},{10,8},{9,1... | collective-permute-start | bytes 589832 | tf_op jit(solution)/shard_map/ppermute | solution.py:404
  71.5 2.4 %command_rows.4.refs_6_ = bf16[128,1024]{1,0:T(8,128)(2,1)S(1)} custom-call(bf16[128,768]{1,0:T(8,128)(2,1)S(1)} %pad_maximum_fusion.1.own_ref.refs_0_, bf16[128,768]{1,0:T(8,128)(2,1)S(1)} %collective-permute-done.20.refs_1_, bf16[128,768]{1,0:T(8,128)(2,1)S(1)} %collective-permute-done.21.refs_2_, bf16[128,768]{1,0:T(8,128)(2,1)S(1)} %collective-permute-done.22.refs_3_, ...), custom_call_target="tpu_custom_call" | custom-call | flops 2147483648 | bytes 524288 | tf_op jit(solution)/shard_map/command_rows/pallas_call | solution.py:362
  73.8 2.5 %collective-permute-done.23.refs_1_ = bf16[128,768]{1,0:T(8,128)(2,1)S(1)} collective-permute-done((bf16[128,768]{1,0:T(8,128)(2,1)S(1)}, bf16[128,768]{1,0:T(8,128)(2,1)S(1)}, u32[]{:S(2)}, u32[]{:S(2)}) %collective-permute-start.23) | collective-permute-done | bytes 196640 | tf_op jit(solution)/shard_map/ppermute | solution.py:404
  76.8 2.8 %collective-permute-done.17.refs_0_ = bf16[128,768]{1,0:T(8,128)(2,1)S(1)} collective-permute-done((bf16[128,768]{1,0:T(8,128)(2,1)S(1)}, bf16[128,768]{1,0:T(8,128)(2,1)S(1)}, u32[]{:S(2)}, u32[]{:S(2)}) %collective-permute-start.17) | collective-permute-done | bytes 196640 | tf_op jit(solution)/shard_map/ppermute | solution.py:404
  80.6 2.4 %command_rows.6.refs_8_ = bf16[128,1024]{1,0:T(8,128)(2,1)S(1)} custom-call(bf16[128,768]{1,0:T(8,128)(2,1)S(1)} %collective-permute-done.26.refs_0_, bf16[128,768]{1,0:T(8,128)(2,1)S(1)} %collective-permute-done.27.refs_1_, bf16[128,768]{1,0:T(8,128)(2,1)S(1)} %collective-permute-done.28.refs_2_, bf16[128,768]{1,0:T(8,128)(2,1)S(1)} %collective-permute-done.29.refs_3_, ...), custom_call_target="tpu_custom_call" | custom-call | flops 2147483648 | bytes 524288 | tf_op jit(solution)/shard_map/command_rows/pallas_call | solution.py:362
  83.0 2.4 %command_rows.5.refs_7_ = bf16[128,1024]{1,0:T(8,128)(2,1)S(1)} custom-call(bf16[128,768]{1,0:T(8,128)(2,1)S(1)} %collective-permute-done.15.other_ref.refs_0_, bf16[128,768]{1,0:T(8,128)(2,1)S(1)} %collective-permute-done.23.refs_1_, bf16[128,768]{1,0:T(8,128)(2,1)S(1)} %collective-permute-done.24.refs_2_, ...), custom_call_target="tpu_custom_call" | custom-call | flops 2147483648 | bytes 524288 | tf_op jit(solution)/shard_map/command_rows/pallas_call | solution.py:362
  85.4 2.3 %command_rows.7 = bf16[512,1024]{1,0:T(8,128)(2,1)} custom-call(bf16[128,768]{1,0:T(8,128)(2,1)S(1)} %collective-permute-done.17.refs_0_, bf16[128,768]{1,0:T(8,128)(2,1)S(1)} %collective-permute-done.18.refs_1_, bf16[768,2048]{1,0:T(8,128)(2,1)S(1)} %tap_matrix.5.refs_5_.refs_2_, bf16[768,2048]{1,0:T(8,128)(2,1)S(1)} %tap_matrix.6.refs_7_.refs_3_, ...), custom_call_target="tpu_custom_call" | custom-call | flops 2147483648 | bytes 524288 | tf_op jit(solution)/shard_map/command_rows/pallas_call | solution.py:362
  (62 shorter events, 10.2 us)
Async XLA Ops:
  1.0 10.5 %collective-permute-start = (bf16[32,1024]{1,0:T(8,128)(2,1)S(1)}, bf16[32,1024]{1,0:T(8,128)(2,1)S(1)}, u32[]{:S(2)}, u32[]{:S(2)}) collective-permute-start(bf16[32,1024]{1,0:T(8,128)(2,1)S(1)} %get-tuple-element.58), channel_id=1, source_target_pairs={{0,4},{4,0},{8,12},{12,8},{1,5},{5,1},{9,13},{13,9},{2,6},{6,2},{1... | collective-permute-start | bytes 196616 | tf_op jit(solution)/shard_map/ppermute | solution.py:404
  4.1 7.4 %collective-permute-start.1 = (bf16[32,1024]{1,0:T(8,128)(2,1)S(1)}, bf16[32,1024]{1,0:T(8,128)(2,1)S(1)}, u32[]{:S(2)}, u32[]{:S(2)}) collective-permute-start(bf16[32,1024]{1,0:T(8,128)(2,1)S(1)} %get-tuple-element.60), channel_id=1, source_target_pairs={{0,8},{4,12},{8,0},{12,4},{1,9},{5,13},{9,1},{13,5},{2,10},{6,14},... | collective-permute-start | bytes 196616 | tf_op jit(solution)/shard_map/ppermute | solution.py:404
  6.7 6.1 %collective-permute-start.2 = (bf16[32,1024]{1,0:T(8,128)(2,1)S(1)}, bf16[32,1024]{1,0:T(8,128)(2,1)S(1)}, u32[]{:S(2)}, u32[]{:S(2)}) collective-permute-start(bf16[32,1024]{1,0:T(8,128)(2,1)S(1)} %get-tuple-element.57), channel_id=1, source_target_pairs={{0,12},{4,8},{8,4},{12,0},{1,13},{5,9},{9,5},{13,1},{2,14},{6,10},... | collective-permute-start | bytes 196616 | tf_op jit(solution)/shard_map/ppermute | solution.py:404
  13.4 6.0 %collective-permute-start.3 = (bf16[32,1024]{1,0:T(8,128)(2,1)S(1)}, bf16[32,1024]{1,0:T(8,128)(2,1)S(1)}, u32[]{:S(2)}, u32[]{:S(2)}) collective-permute-start(bf16[32,1024]{1,0:T(8,128)(2,1)S(1)} %get-tuple-element.36), channel_id=1, source_target_pairs={{0,4},{4,0},{8,12},{12,8},{1,5},{5,1},{9,13},{13,9},{2,6},{6,2},{1... | collective-permute-start | bytes 196616 | tf_op jit(solution)/shard_map/ppermute | solution.py:404
  13.5 5.9 %collective-permute-start.4 = (bf16[32,1024]{1,0:T(8,128)(2,1)S(1)}, bf16[32,1024]{1,0:T(8,128)(2,1)S(1)}, u32[]{:S(2)}, u32[]{:S(2)}) collective-permute-start(bf16[32,1024]{1,0:T(8,128)(2,1)S(1)} %get-tuple-element.37), channel_id=1, source_target_pairs={{0,8},{4,12},{8,0},{12,4},{1,9},{5,13},{9,1},{13,5},{2,10},{6,14},... | collective-permute-start | bytes 196616 | tf_op jit(solution)/shard_map/ppermute | solution.py:404
  16.6 6.1 %collective-permute-start.5 = (bf16[32,1024]{1,0:T(8,128)(2,1)S(1)}, bf16[32,1024]{1,0:T(8,128)(2,1)S(1)}, u32[]{:S(2)}, u32[]{:S(2)}) collective-permute-start(bf16[32,1024]{1,0:T(8,128)(2,1)S(1)} %get-tuple-element.38), channel_id=1, source_target_pairs={{0,12},{4,8},{8,4},{12,0},{1,13},{5,9},{9,5},{13,1},{2,14},{6,10},... | collective-permute-start | bytes 196616 | tf_op jit(solution)/shard_map/ppermute | solution.py:404
  22.7 6.4 %collective-permute-start.10 = (bf16[4,32,1024]{2,1,0:T(8,128)(2,1)S(1)}, bf16[4,32,1024]{2,1,0:T(8,128)(2,1)S(1)}, u32[]{:S(2)}, u32[]{:S(2)}) collective-permute-start(bf16[4,32,1024]{2,1,0:T(8,128)(2,1)S(1)} %pad_maximum_fusion.own_ref), channel_id=1, source_target_pairs={{0,2},{2,0},{1,3},{3,1},{4,6},{6,4},{5,7},{7,5},{8,10},{10,8},{9,1... | collective-permute-start | bytes 786440 | tf_op jit(solution)/shard_map/ppermute | solution.py:404
  24.3 4.9 %collective-permute-start.6 = (bf16[4,32,1024]{2,1,0:T(8,128)(2,1)S(1)}, bf16[4,32,1024]{2,1,0:T(8,128)(2,1)S(1)}, u32[]{:S(2)}, u32[]{:S(2)}) collective-permute-start(bf16[4,32,1024]{2,1,0:T(8,128)(2,1)S(1)} %pad_maximum_fusion.own_ref), channel_id=1, source_target_pairs={{0,1},{1,0},{2,3},{3,2},{4,5},{5,4},{6,7},{7,6},{8,9},{9,8},{10,11... | collective-permute-start | bytes 786440 | tf_op jit(solution)/shard_map/ppermute | solution.py:404
  29.2 6.3 %collective-permute-start.11 = (bf16[4,32,1024]{2,1,0:T(8,128)(2,1)S(1)}, bf16[4,32,1024]{2,1,0:T(8,128)(2,1)S(1)}, u32[]{:S(2)}, u32[]{:S(2)}) collective-permute-start(bf16[4,32,1024]{2,1,0:T(8,128)(2,1)S(1)} %collective-permute-done.10.own_ref), channel_id=1, source_target_pairs={{0,1},{1,0},{2,3},{3,2},{4,5},{5,4},{6,7},{7,6},{8,9},{9,8},{10,11... | collective-permute-start | bytes 786440 | tf_op jit(solution)/shard_map/ppermute | solution.py:404
  31.0 33.9 %copy-start.4 = (s32[1,4,4,2048]{3,2,1,0:T(4,128)S(1)}, s32[1,4,4,2048]{3,2,1,0:T(4,128)}, u32[]{:S(2)}) copy-start(s32[1,4,4,2048]{3,2,1,0:T(4,128)} %param.13) | copy-start | bytes 393220
  31.0 33.9 %copy-start.6 = (f32[1,4,4,2048]{3,2,1,0:T(4,128)S(1)}, f32[1,4,4,2048]{3,2,1,0:T(4,128)}, u32[]{:S(2)}) copy-start(f32[1,4,4,2048]{3,2,1,0:T(4,128)} %param.14) | copy-start | bytes 393220
  31.0 8.1 %collective-permute-start.7 = (bf16[64,768]{1,0:T(8,128)(2,1)S(1)}, bf16[64,768]{1,0:T(8,128)(2,1)S(1)}, u32[]{:S(2)}, u32[]{:S(2)}) collective-permute-start(bf16[64,768]{1,0:T(8,128)(2,1)S(1)} %get-tuple-element.44), channel_id=1, source_target_pairs={{0,4},{4,0},{8,12},{12,8},{1,5},{5,1},{9,13},{13,9},{2,6},{6,2},{1... | collective-permute-start | bytes 294920 | tf_op jit(solution)/shard_map/ppermute | solution.py:404
  31.1 10.9 %collective-permute-start.8 = (bf16[64,768]{1,0:T(8,128)(2,1)S(1)}, bf16[64,768]{1,0:T(8,128)(2,1)S(1)}, u32[]{:S(2)}, u32[]{:S(2)}) collective-permute-start(bf16[64,768]{1,0:T(8,128)(2,1)S(1)} %get-tuple-element.45), channel_id=1, source_target_pairs={{0,8},{4,12},{8,0},{12,4},{1,9},{5,13},{9,1},{13,5},{2,10},{6,14},... | collective-permute-start | bytes 294920 | tf_op jit(solution)/shard_map/ppermute | solution.py:404
  32.9 9.1 %collective-permute-start.9 = (bf16[64,768]{1,0:T(8,128)(2,1)S(1)}, bf16[64,768]{1,0:T(8,128)(2,1)S(1)}, u32[]{:S(2)}, u32[]{:S(2)}) collective-permute-start(bf16[64,768]{1,0:T(8,128)(2,1)S(1)} %get-tuple-element.46), channel_id=1, source_target_pairs={{0,12},{4,8},{8,4},{12,0},{1,13},{5,9},{9,5},{13,1},{2,14},{6,10},... | collective-permute-start | bytes 294920 | tf_op jit(solution)/shard_map/ppermute | solution.py:404
  37.2 6.4 %collective-permute-start.12 = (bf16[64,768]{1,0:T(8,128)(2,1)S(1)}, bf16[64,768]{1,0:T(8,128)(2,1)S(1)}, u32[]{:S(2)}, u32[]{:S(2)}) collective-permute-start(bf16[64,768]{1,0:T(8,128)(2,1)S(1)} %get-tuple-element.48), channel_id=1, source_target_pairs={{0,4},{4,0},{8,12},{12,8},{1,5},{5,1},{9,13},{13,9},{2,6},{6,2},{1... | collective-permute-start | bytes 294920 | tf_op jit(solution)/shard_map/ppermute | solution.py:404
  37.3 13.1 %collective-permute-start.13 = (bf16[64,768]{1,0:T(8,128)(2,1)S(1)}, bf16[64,768]{1,0:T(8,128)(2,1)S(1)}, u32[]{:S(2)}, u32[]{:S(2)}) collective-permute-start(bf16[64,768]{1,0:T(8,128)(2,1)S(1)} %get-tuple-element.49), channel_id=1, source_target_pairs={{0,8},{4,12},{8,0},{12,4},{1,9},{5,13},{9,1},{13,5},{2,10},{6,14},... | collective-permute-start | bytes 294920 | tf_op jit(solution)/shard_map/ppermute | solution.py:404
  39.1 11.3 %collective-permute-start.14 = (bf16[64,768]{1,0:T(8,128)(2,1)S(1)}, bf16[64,768]{1,0:T(8,128)(2,1)S(1)}, u32[]{:S(2)}, u32[]{:S(2)}) collective-permute-start(bf16[64,768]{1,0:T(8,128)(2,1)S(1)} %get-tuple-element.50), channel_id=1, source_target_pairs={{0,12},{4,8},{8,4},{12,0},{1,13},{5,9},{9,5},{13,1},{2,14},{6,10},... | collective-permute-start | bytes 294920 | tf_op jit(solution)/shard_map/ppermute | solution.py:404
  50.5 9.7 %collective-permute-start.15 = (bf16[128,768]{1,0:T(8,128)(2,1)S(1)}, bf16[128,768]{1,0:T(8,128)(2,1)S(1)}, u32[]{:S(2)}, u32[]{:S(2)}) collective-permute-start(bf16[128,768]{1,0:T(8,128)(2,1)S(1)} %pad_maximum_fusion.1.own_ref.refs_0_), channel_id=1, source_target_pairs={{0,12},{4,8},{8,4},{12,0},{1,13},{5,9},{9,5},{13,1},{2,14},{6,10},... | collective-permute-start | bytes 589832 | tf_op jit(solution)/shard_map/ppermute | solution.py:404
  52.6 10.8 %collective-permute-start.26 = (bf16[128,768]{1,0:T(8,128)(2,1)S(1)}, bf16[128,768]{1,0:T(8,128)(2,1)S(1)}, u32[]{:S(2)}, u32[]{:S(2)}) collective-permute-start(bf16[128,768]{1,0:T(8,128)(2,1)S(1)} %pad_maximum_fusion.1.own_ref.refs_0_), channel_id=1, source_target_pairs={{0,4},{4,0},{8,12},{12,8},{1,5},{5,1},{9,13},{13,9},{2,6},{6,2},{1... | collective-permute-start | bytes 589832 | tf_op jit(solution)/shard_map/ppermute | solution.py:404
  53.6 11.3 %collective-permute-start.20 = (bf16[128,768]{1,0:T(8,128)(2,1)S(1)}, bf16[128,768]{1,0:T(8,128)(2,1)S(1)}, u32[]{:S(2)}, u32[]{:S(2)}) collective-permute-start(bf16[128,768]{1,0:T(8,128)(2,1)S(1)} %pad_maximum_fusion.1.own_ref.refs_0_), channel_id=1, source_target_pairs={{0,2},{2,0},{1,3},{3,1},{4,6},{6,4},{5,7},{7,5},{8,10},{10,8},{9,1... | collective-permute-start | bytes 589832 | tf_op jit(solution)/shard_map/ppermute | solution.py:404
  55.1 13.4 %collective-permute-start.21 = (bf16[128,768]{1,0:T(8,128)(2,1)S(1)}, bf16[128,768]{1,0:T(8,128)(2,1)S(1)}, u32[]{:S(2)}, u32[]{:S(2)}) collective-permute-start(bf16[128,768]{1,0:T(8,128)(2,1)S(1)} %pad_maximum_fusion.1.own_ref.refs_0_), channel_id=1, source_target_pairs={{0,1},{1,0},{2,3},{3,2},{4,5},{5,4},{6,7},{7,6},{8,9},{9,8},{10,11... | collective-permute-start | bytes 589832 | tf_op jit(solution)/shard_map/ppermute | solution.py:404
  60.2 8.8 %collective-permute-start.16 = (bf16[128,768]{1,0:T(8,128)(2,1)S(1)}, bf16[128,768]{1,0:T(8,128)(2,1)S(1)}, u32[]{:S(2)}, u32[]{:S(2)}) collective-permute-start(bf16[128,768]{1,0:T(8,128)(2,1)S(1)} %pass_on.1), channel_id=1, source_target_pairs={{0,8},{4,0},{8,12},{12,4},{1,9},{5,1},{9,13},{13,5},{2,10},{6,2},{... | collective-permute-start | bytes 589832 | tf_op jit(solution)/shard_map/ppermute | solution.py:462
  63.4 6.5 %collective-permute-start.27 = (bf16[128,768]{1,0:T(8,128)(2,1)S(1)}, bf16[128,768]{1,0:T(8,128)(2,1)S(1)}, u32[]{:S(2)}, u32[]{:S(2)}) collective-permute-start(bf16[128,768]{1,0:T(8,128)(2,1)S(1)} %collective-permute-done.26.refs_0_), channel_id=1, source_target_pairs={{0,2},{2,0},{1,3},{3,1},{4,6},{6,4},{5,7},{7,5},{8,10},{10,8},{9,1... | collective-permute-start | bytes 589832 | tf_op jit(solution)/shard_map/ppermute | solution.py:404
  64.9 6.5 %collective-permute-start.22 = (bf16[128,768]{1,0:T(8,128)(2,1)S(1)}, bf16[128,768]{1,0:T(8,128)(2,1)S(1)}, u32[]{:S(2)}, u32[]{:S(2)}) collective-permute-start(bf16[128,768]{1,0:T(8,128)(2,1)S(1)} %collective-permute-done.20.refs_1_), channel_id=1, source_target_pairs={{0,1},{1,0},{2,3},{3,2},{4,5},{5,4},{6,7},{7,6},{8,9},{9,8},{10,11... | collective-permute-start | bytes 589832 | tf_op jit(solution)/shard_map/ppermute | solution.py:404
  68.0 12.6 %collective-permute-start.28 = (bf16[128,768]{1,0:T(8,128)(2,1)S(1)}, bf16[128,768]{1,0:T(8,128)(2,1)S(1)}, u32[]{:S(2)}, u32[]{:S(2)}) collective-permute-start(bf16[128,768]{1,0:T(8,128)(2,1)S(1)} %collective-permute-done.26.refs_0_), channel_id=1, source_target_pairs={{0,1},{1,0},{2,3},{3,2},{4,5},{5,4},{6,7},{7,6},{8,9},{9,8},{10,11... | collective-permute-start | bytes 589832 | tf_op jit(solution)/shard_map/ppermute | solution.py:404
  68.5 7.8 %collective-permute-start.23 = (bf16[128,768]{1,0:T(8,128)(2,1)S(1)}, bf16[128,768]{1,0:T(8,128)(2,1)S(1)}, u32[]{:S(2)}, u32[]{:S(2)}) collective-permute-start(bf16[128,768]{1,0:T(8,128)(2,1)S(1)} %collective-permute-done.15.other_ref.refs_0_), channel_id=1, source_target_pairs={{0,2},{2,0},{1,3},{3,1},{4,6},{6,4},{5,7},{7,5},{8,10},{10,8},{9,1... | collective-permute-start | bytes 589832 | tf_op jit(solution)/shard_map/ppermute | solution.py:404
  69.0 7.2 %collective-permute-start.19 = (bf16[128,768]{1,0:T(8,128)(2,1)S(1)}, bf16[128,768]{1,0:T(8,128)(2,1)S(1)}, u32[]{:S(2)}, u32[]{:S(2)}) collective-permute-start(bf16[128,768]{1,0:T(8,128)(2,1)S(1)} %collective-permute-done.16.own_ref), channel_id=1, source_target_pairs={{0,1},{1,0},{2,3},{3,2},{4,5},{5,4},{6,7},{7,6},{8,9},{9,8},{10,11... | collective-permute-start | bytes 589832 | tf_op jit(solution)/shard_map/ppermute | solution.py:404
  70.0 9.7 %collective-permute-start.17 = (bf16[128,768]{1,0:T(8,128)(2,1)S(1)}, bf16[128,768]{1,0:T(8,128)(2,1)S(1)}, u32[]{:S(2)}, u32[]{:S(2)}) collective-permute-start(bf16[128,768]{1,0:T(8,128)(2,1)S(1)} %collective-permute-done.16.own_ref), channel_id=1, source_target_pairs={{0,2},{2,0},{1,3},{3,1},{4,6},{6,4},{5,7},{7,5},{8,10},{10,8},{9,1... | collective-permute-start | bytes 589832 | tf_op jit(solution)/shard_map/ppermute | solution.py:404
  71.4 9.2 %collective-permute-start.29 = (bf16[128,768]{1,0:T(8,128)(2,1)S(1)}, bf16[128,768]{1,0:T(8,128)(2,1)S(1)}, u32[]{:S(2)}, u32[]{:S(2)}) collective-permute-start(bf16[128,768]{1,0:T(8,128)(2,1)S(1)} %collective-permute-done.27.refs_1_), channel_id=1, source_target_pairs={{0,1},{1,0},{2,3},{3,2},{4,5},{5,4},{6,7},{7,6},{8,9},{9,8},{10,11... | collective-permute-start | bytes 589832 | tf_op jit(solution)/shard_map/ppermute | solution.py:404
  76.3 6.7 %collective-permute-start.24 = (bf16[128,768]{1,0:T(8,128)(2,1)S(1)}, bf16[128,768]{1,0:T(8,128)(2,1)S(1)}, u32[]{:S(2)}, u32[]{:S(2)}) collective-permute-start(bf16[128,768]{1,0:T(8,128)(2,1)S(1)} %collective-permute-done.15.other_ref.refs_0_), channel_id=1, source_target_pairs={{0,1},{1,0},{2,3},{3,2},{4,5},{5,4},{6,7},{7,6},{8,9},{9,8},{10,11... | collective-permute-start | bytes 589832 | tf_op jit(solution)/shard_map/ppermute | solution.py:404
  76.3 6.7 %collective-permute-start.25 = (bf16[128,768]{1,0:T(8,128)(2,1)S(1)}, bf16[128,768]{1,0:T(8,128)(2,1)S(1)}, u32[]{:S(2)}, u32[]{:S(2)}) collective-permute-start(bf16[128,768]{1,0:T(8,128)(2,1)S(1)} %collective-permute-done.23.refs_1_), channel_id=1, source_target_pairs={{0,1},{1,0},{2,3},{3,2},{4,5},{5,4},{6,7},{7,6},{8,9},{9,8},{10,11... | collective-permute-start | bytes 589832 | tf_op jit(solution)/shard_map/ppermute | solution.py:404
  79.6 5.8 %collective-permute-start.18 = (bf16[128,768]{1,0:T(8,128)(2,1)S(1)}, bf16[128,768]{1,0:T(8,128)(2,1)S(1)}, u32[]{:S(2)}, u32[]{:S(2)}) collective-permute-start(bf16[128,768]{1,0:T(8,128)(2,1)S(1)} %collective-permute-done.17.refs_0_), channel_id=1, source_target_pairs={{0,1},{1,0},{2,3},{3,2},{4,5},{5,4},{6,7},{7,6},{8,9},{9,8},{10,11... | collective-permute-start | bytes 589832 | tf_op jit(solution)/shard_map/ppermute | solution.py:404
  (5 other events, 51.5 us)
